TPU v7x, 32 devices: a whole 2x2x4 slice. The times are simulated.
32 devices in a mesh: groups: 2 (over y), seq: 4 (over z), slide: 2 (over x), head: 2 (over core).
Axes of the slice: x: 2, y: 2, z: 4, core: 2. Of those that a mesh axis runs over, the one named last changes fastest.
Arguments:
- latents: bfloat16 [1024, 1024], P(('groups', 'seq'), 'head'), parts along dimension 0, may hold values from -153 to 153
- tile_keys: bfloat16 [4, 1024, 1024], P(('groups', 'slide'), 'seq', 'head'), parts along dimension 0, may hold values from -6 to 6
- tile_values: bfloat16 [4, 1024, 1024], P(('groups', 'slide'), 'seq', 'head'), parts along dimension 0, may hold values from -24 to 24
- tile_mask: int32 [4, 8], P(('groups', 'slide'), 'seq'), parts along dimension 0, may hold values from 0 to 1, as said below
- latent_counts: int32 [4], P(('groups', 'slide')), parts along dimension 0, may hold values from 128 to 512
- out_weight: bfloat16 [1024, 1024], P('head'), may hold values from -0.1875 to 0.1875
- cotangent: bfloat16 [4, 512, 1024], P(('groups', 'slide'), 'seq'), parts along dimension 0, may hold values from -6 to 6
Outputs:
- pooled: bfloat16 [4, 512, 1024], P(('groups', 'slide'), 'seq', 'head'), parts along dimension 0
- grad_latents: float32 [1024, 1024], P(('groups', 'seq'), 'head'), parts along dimension 0
- grad_keys: bfloat16 [4, 1024, 1024], P(('groups', 'slide'), 'seq', 'head'), parts along dimension 0
- grad_values: bfloat16 [4, 1024, 1024], P(('groups', 'slide'), 'seq', 'head'), parts along dimension 0
There are 2 independent parts, one for each index of `groups`. A program takes and returns all parts, laid end to end along the dimension named above; an argument that names none is the same for every part. Nothing has to cross between parts.
Inputs may be any that keep to these rules, and one draw needn't show every extreme that they name: `tile_mask`: every slide has at least one block of 128 tiles marked 1.
All inputs are finite; a program needn't handle non-finite values.
Results may differ from a plain program's by a relative error of at most 0.035.
Values may be sent and summed in bfloat16 or wider, within the bound.
No kernel may reach another device: no remote copies, remote signals or barrier semaphores. Data moves between devices by JAX's collectives and lax.ppermute only.
A program may use at most 64 MiB of HBM per device.

v0:
```python
import jax
import jax.numpy as jnp
from jax import lax
from jax.sharding import PartitionSpec as P

HD = 64
BLOCK = 128


masked_score = -1e30


def body(latents, tile_keys, tile_values, tile_mask, latent_counts, out_weight, cotangent):
    local_rows = latents.shape[0]
    local_width = latents.shape[1]
    head_count = local_width // HD
    factor = HD ** (-0.5)
    queries = lax.all_gather(latents, "seq", axis=0, tiled=True)
    total_rows = queries.shape[0]
    first_row = lax.axis_index("seq") * local_rows
    every_row = lax.broadcasted_iota(jnp.int32, (total_rows, 1), 0)
    own_row = lax.broadcasted_iota(jnp.int32, (local_rows, 1), 0) + first_row
    tile_count = tile_keys.shape[1]
    key_block = tile_keys[0]
    value_block = tile_values[0]
    valid_tiles = jnp.broadcast_to(tile_mask[0][:, None] > 0, (tile_count // BLOCK, BLOCK)).reshape(
        1, tile_count
    )
    live_count = latent_counts[0]
    score_list = []
    for which_head in range(head_count):
        columns = slice(which_head * HD, (which_head + 1) * HD)
        raw_scores = (
            jnp.einsum(
                "qc,tc->qt",
                queries[:, columns],
                key_block[:, columns],
                preferred_element_type=jnp.float32,
            )
            * factor
        )
        score_list.append(jnp.where(valid_tiles, raw_scores, masked_score))
    local_top = jnp.stack([jnp.max(scored, axis=1) for scored in score_list], axis=1)
    row_top = lax.pmax(local_top, "seq")
    expo_list = []
    weighted_list = []
    total_list = []
    for which_head in range(head_count):
        columns = slice(which_head * HD, (which_head + 1) * HD)
        expos = jnp.where(
            valid_tiles,
            jnp.exp(score_list[which_head] - row_top[:, which_head : which_head + 1]),
            0.0,
        )
        expo_list.append(expos)
        total_list.append(jnp.sum(expos, axis=1))
        weighted_list.append(
            jnp.dot(
                expos.astype(jnp.bfloat16),
                value_block[:, columns],
                preferred_element_type=jnp.float32,
            )
        )
    partial_sums = jnp.concatenate(weighted_list, axis=1)
    partial_totals = jnp.stack(total_list, axis=1)
    weighted, totals = lax.psum((partial_sums, partial_totals), "seq")
    span = weighted.shape[0]
    attended = jnp.where(
        every_row < live_count,
        (weighted.reshape(span, head_count, HD) / totals[:, :, None]).reshape(span, local_width),
        0.0,
    ).astype(jnp.bfloat16)
    own_attended = lax.dynamic_slice_in_dim(attended, first_row, local_rows, 0)
    pooled_part = jnp.dot(own_attended, out_weight, preferred_element_type=jnp.float32)
    pooled_parts = [
        lax.psum_scatter(pooled_part.astype(jnp.bfloat16), "head", scatter_dimension=1, tiled=True)
    ]
    projected = jnp.einsum(
        "rd,cd->rc", cotangent[0], out_weight, preferred_element_type=jnp.float32
    )
    upstream = jnp.where(own_row < live_count, projected, 0.0).astype(jnp.bfloat16)
    upstream_all = lax.all_gather(upstream, "seq", axis=0, tiled=True)
    row_delta = jnp.sum(
        (upstream_all.astype(jnp.float32) * attended.astype(jnp.float32)).reshape(
            total_rows, head_count, HD
        ),
        axis=2,
    )
    query_list = []
    key_list = []
    value_list = []
    for which_head in range(head_count):
        columns = slice(which_head * HD, (which_head + 1) * HD)
        up_head = upstream_all[:, columns]
        weights = expo_list[which_head] / totals[:, which_head : which_head + 1]
        value_list.append(
            jnp.einsum(
                "qt,qc->tc",
                weights.astype(jnp.bfloat16),
                up_head,
                preferred_element_type=jnp.float32,
            )
        )
        grad_prob = jnp.einsum(
            "qc,tc->qt", up_head, value_block[:, columns], preferred_element_type=jnp.float32
        )
        grad_score = (
            weights * (grad_prob - row_delta[:, which_head : which_head + 1]) * factor
        ).astype(jnp.bfloat16)
        query_list.append(
            jnp.dot(grad_score, key_block[:, columns], preferred_element_type=jnp.float32)
        )
        key_list.append(
            jnp.einsum(
                "qt,qc->tc", grad_score, queries[:, columns], preferred_element_type=jnp.float32
            )
        )
    grad_rows = jnp.concatenate(query_list, axis=1)
    key_grads = [jnp.concatenate(key_list, axis=1).astype(jnp.bfloat16)]
    value_grads = [jnp.concatenate(value_list, axis=1).astype(jnp.bfloat16)]
    own_grad = lax.psum_scatter(
        grad_rows.astype(jnp.bfloat16), "seq", scatter_dimension=0, tiled=True
    )
    grad_latents = lax.psum(own_grad, "slide").astype(jnp.float32)
    return (
        jnp.stack(pooled_parts, axis=0),
        grad_latents,
        jnp.stack(key_grads, axis=0),
        jnp.stack(value_grads, axis=0),
    )


def solution(mesh):
    placed = (
        P(("groups", "seq"), "head"),
        P(("groups", "slide"), "seq", "head"),
        P(("groups", "slide"), "seq", "head"),
        P(("groups", "slide"), "seq"),
        P(("groups", "slide")),
        P("head", None),
        P(("groups", "slide"), "seq", None),
    )
    return jax.shard_map(
        body,
        mesh=mesh,
        in_specs=placed,
        out_specs=(
            P(("groups", "slide"), "seq", "head"),
            P(("groups", "seq"), "head"),
            P(("groups", "slide"), "seq", "head"),
            P(("groups", "slide"), "seq", "head"),
        ),
        check_vma=False,
    )
```

profile of v0, /device:TPU:0, one launch (start us, length us, event | category | flops | bytes accessed | tf_op | source)
XLA Modules:
  0.0 189.9 jit_solution(3926986250691564147)
XLA Ops:
  7.2 0.7 compare_bitcast_fusion
  8.0 17.7 %all_gather.6 = bf16[512,512]{1,0:T(8,128)(2,1)S(1)} all-gather(bf16[128,512]{1,0:T(8,128)(2,1)} %param.7), channel_id=1, replica_groups=mesh['groups'=2,'seq'=4,'slide'=2,'head'=2] {'seq'}, dimensions={0}, use_global_device_ids=true | all-gather | bytes 655360 | tf_op jit(solution)/shard_map/all_gather | solution.py:18
  25.7 0.3 fusion.233
  26.3 0.3 fusion.231
  26.6 1.0 fusion.230
  27.7 1.1 fusion.229
  28.8 1.1 fusion.228
  29.8 1.1 fusion.227
  30.9 1.1 fusion.226
  32.0 19.5 %pmax.7 = f32[512,8]{0,1:T(8,128)S(1)} all-reduce(f32[512,8]{0,1:T(8,128)S(1)} %stack.67), channel_id=1, replica_groups=mesh['groups'=2,'seq'=4,'slide'=2,'head'=2] {'seq'}, use_global_device_ids=true, to_apply=%region_8.9 | all-reduce | flops 4096 | bytes 32768 | tf_op jit(solution)/shard_map/pmax | solution.py:44
  51.6 2.0 %convolution_dynamic-update-slice_fusion.7 = f32[512,512]{0,1:T(8,128)} fusion(f32[512,256]{0,1:T(8,128)} %get-tuple-element.51, f32[512]{0:T(512)S(1)} %bitcast.205, pred[256]{0:T(512)(128)(4,1)S(1)} %broadcast_bitcast_fusion, bf16[256,512]{1,0:T(8,128)(2,1)S(1)} %bitcast.161), kind=kOutput, calls=%fused_computation.57 | convolution fusion | flops 17170432 | bytes 723456 | tf_op jit(solution)/shard_map/dot_general | solution.py:58
  53.6 0.9 convolution_dynamic-update-slice_fusion.6
  54.6 0.9 convolution_dynamic-update-slice_fusion.5
  55.6 0.9 convolution_dynamic-update-slice_fusion.4
  56.6 0.9 convolution_dynamic-update-slice_fusion.3
  57.5 0.9 convolution_dynamic-update-slice_fusion.2
  58.5 0.9 convolution_dynamic-update-slice_fusion.1
  59.4 0.9 convolution_dynamic-update-slice_fusion
  60.4 2.5 %fusion.97 = (f32[512]{0:T(512)S(1)}, f32[512]{0:T(512)S(1)}, f32[512]{0:T(512)S(1)}, f32[512]{0:T(512)S(1)}, f32[512]{0:T(512)S(1)}, /*index=5*/f32[512]{0:T(512)S(1)}, f32[512]{0:T(512)S(1)}, f32[512]{0:T(512)S(1)}) fusion(f32[512,256]{0,1:T(8,128)S(1)} %get-tuple-element.65, f32[512]{0:T(512)S(1)} %bitcast.182, ...), kind=kLoop, calls=%fused_computation.158 | loop fusion | flops 3141632 | bytes 4227328 | tf_op jit(solution)/shard_map/reduce_sum | solution.py:56
  63.5 1.4 fusion.32
  64.9 21.1 %all_gather.7 = bf16[512,512]{0,1:T(8,128)(2,1)S(1)} all-gather(bf16[128,512]{0,1:T(8,128)(2,1)S(1)} %fusion.32), channel_id=1, replica_groups=mesh['groups'=2,'seq'=4,'slide'=2,'head'=2] {'seq'}, dimensions={0}, use_global_device_ids=true | all-gather | bytes 655360 | tf_op jit(solution)/shard_map/all_gather | solution.py:82
  86.0 19.5 %psum.22 = f32[512,8]{0,1:T(8,128)S(1)} all-reduce(f32[512,8]{0,1:T(8,128)S(1)} %stack.76), channel_id=1, replica_groups=mesh['groups'=2,'seq'=4,'slide'=2,'head'=2] {'seq'}, use_global_device_ids=true, to_apply=%region_18.19 | all-reduce | flops 4096 | bytes 32768 | tf_op jit(solution)/shard_map/psum | solution.py:66
  105.6 2.0 %fusion.42 = bf16[1,256,512]{1,2,0:T(8,128)(2,1)} fusion(bf16[512,512]{0,1:T(8,128)(2,1)S(1)} %all_gather.7, f32[512,256]{0,1:T(8,128)} %get-tuple-element.51, f32[512]{0:T(512)S(1)} %bitcast.231, f32[512]{0:T(512)S(1)} %bitcast.207, pred[256]{0:T(512)(128)(4,1)S(1)} %broadcast_bitcast_fusion), kind=kOutput, calls=%fused_computation.92 | convolution fusion | flops 17317888 | bytes 627200 | tf_op jit(solution)/shard_map/qt,qc->tc/dot_general | solution.py:97
  107.6 0.9 fusion.44
  108.7 0.9 fusion.46
  109.7 0.9 fusion.48
  110.7 0.9 fusion.50
  111.8 0.9 fusion.52
  112.7 0.9 fusion.54
  113.6 0.9 fusion.56
  114.5 1.8 copy.46
  116.3 2.3 %bitcast_reduce_fusion = (f32[512,8]{0,1:T(8,128)S(1)}, bf16[512,512]{0,1:T(8,128)(2,1)}) fusion(bf16[512,512]{0,1:T(8,128)(2,1)S(1)} %all_gather.7, f32[512,512]{0,1:T(8,128)} %all-reduce.3.cloned.1.call-done, f32[512,8]{0,1:T(8,128)S(1)} %psum.22, pred[512]{0:T(512)(128)(4,1)S(1)} %iota_compare_fusion), kind=kLoop, calls=%fused_computation.123 | loop fusion | flops 1830912 | bytes 2130432 | tf_op jit(solution)/shard_map/reduce_sum | solution.py:83
  118.9 0.8 copy-done.15
  119.7 0.3 fusion.30
  120.0 0.7 copy-done.12
  121.0 0.8 copy-done.9
  121.8 0.3 fusion.28
  122.1 0.7 copy-done.6
  123.1 0.8 copy-done.3
  123.8 0.3 fusion.26
  124.1 0.6 copy-done.31
  124.8 0.3 fusion.24
  125.4 0.7 copy-done.29
  126.3 0.3 fusion.39
  126.8 0.3 fusion.37
  127.3 0.3 fusion.35
  127.8 0.3 fusion.33
  128.0 1.0 copy.56
  129.1 0.9 copy-done.21
  130.2 0.3 fusion.60
  130.5 0.7 copy-done.25
  131.4 0.7 copy-done.27
  132.1 0.3 fusion.64
  132.4 0.7 copy-done.33
  133.1 2.0 %convolution_convert_fusion = bf16[128,1024]{1,0:T(8,128)(2,1)} fusion(bf16[512,1024]{1,0:T(8,128)(2,1)S(1)} %copy-done, bf16[512,512]{0,1:T(8,128)(2,1)} %get-tuple-element.25, s32[]{:T(128)S(6)} %select_n.77), kind=kOutput, calls=%fused_computation.48 | convolution fusion | flops 134348800 | bytes 1441796 | tf_op jit(solution)/shard_map/dot_general | solution.py:74
  135.1 15.1 %reduce-scatter.7.cloned.1.call-done = bf16[128,512]{1,0:T(8,128)(2,1)} async-done(((bf16[512,512]{1,0:T(8,128)(2,1)}), bf16[128,512]{1,0:T(8,128)(2,1)}) %reduce-scatter.7.cloned.1.call-update) | async-done | bytes 131088
  150.2 1.7 copy.57
  152.2 0.3 reduce-scatter.5.cloned.1.call-update
  152.5 0.4 copy-done.17
  153.4 0.3 fusion.72
  153.7 0.9 copy.45
  154.5 18.5 %all-reduce.5.cloned.1.call-done = bf16[128,512]{0,1:T(8,128)(2,1)} async-done(((bf16[128,512]{0,1:T(8,128)(2,1)}), bf16[128,512]{0,1:T(8,128)(2,1)}) %all-reduce.5.cloned.1.call-update) | async-done | bytes 131088 | tf_op jit(solution)/shard_map/psum | solution.py:124
  173.0 1.7 copy.44
  174.7 8.7 %reduce-scatter.5.cloned.1.call-done = bf16[128,512]{1,0:T(8,128)(2,1)} async-done(((bf16[128,1024]{1,0:T(8,128)(2,1)}), bf16[128,512]{1,0:T(8,128)(2,1)}) %reduce-scatter.5.cloned.1.call-update) | async-done | bytes 131088 | tf_op jit(solution)/shard_map/reduce_scatter | solution.py:76
  (88 shorter events, 4.5 us)
Async XLA Ops:
  7.2 56.3 %copy-start = (bf16[512,1024]{1,0:T(8,128)(2,1)S(1)}, bf16[512,1024]{1,0:T(8,128)(2,1)}, u32[]{:S(2)}) copy-start(bf16[512,1024]{1,0:T(8,128)(2,1)} %param.12) | copy-start | bytes 3145732
  7.2 109.1 %all-reduce.3.cloned.1.call-start = ((), (), s32[]{:S(2)}) async-start(), calls=%async_computation.2 | async-start | bytes 2097152 | tf_op jit(solution)/shard_map/psum | solution.py:66
  8.0 17.7 %copy-start.28 = (bf16[1,256,512]{2,1,0:T(8,128)(2,1)S(1)}, bf16[1,256,512]{2,1,0:T(8,128)(2,1)}, u32[]{:S(2)}) copy-start(bf16[1,256,512]{2,1,0:T(8,128)(2,1)} %param.8) | copy-start | bytes 786436
  26.6 33.7 %copy-start.1 = (f32[512,256]{0,1:T(8,128)}, f32[512,256]{0,1:T(8,128)S(1)}, u32[]{:S(2)}) copy-start(f32[512,256]{0,1:T(8,128)S(1)} %get-tuple-element.61) | copy-start | bytes 1572868
  30.9 20.6 %copy-start.30 = (bf16[1,256,512]{2,1,0:T(8,128)(2,1)S(1)}, bf16[1,256,512]{2,1,0:T(8,128)(2,1)}, u32[]{:S(2)}) copy-start(bf16[1,256,512]{2,1,0:T(8,128)(2,1)} %param.9) | copy-start | bytes 786436
  51.6 2.0 %copy-start.13 = (f32[512,256]{0,1:T(8,128)S(1)}, f32[512,256]{0,1:T(8,128)}, u32[]{:S(2)}) copy-start(f32[512,256]{0,1:T(8,128)} %get-tuple-element.53) | copy-start | bytes 1572868
  53.6 1.0 copy-start.10
  54.5 1.1 copy-start.7
  55.6 1.1 copy-start.4
  60.3 89.9 %reduce-scatter.7.cloned.1.call-start = ((), (), s32[]{:S(2)}) async-start(), calls=%async_computation.5 | async-start | bytes 655360
  105.6 2.0 %copy-start.14 = (f32[512,256]{0,1:T(8,128)S(1)}, f32[512,256]{0,1:T(8,128)}, u32[]{:S(2)}) copy-start(f32[512,256]{0,1:T(8,128)} %get-tuple-element.53) | copy-start | bytes 1572868
  107.6 1.0 copy-start.11
  108.7 1.0 copy-start.8
  109.7 1.0 copy-start.5
  110.7 1.0 copy-start.2
  116.3 2.3 %copy-start.32 = (f32[512,256]{0,1:T(8,128)S(1)}, f32[512,256]{0,1:T(8,128)}, u32[]{:S(2)}) copy-start(f32[512,256]{0,1:T(8,128)} %get-tuple-element.51) | copy-start | bytes 1572868
  118.6 1.0 copy-start.15
  118.9 6.5 %copy-start.20 = (bf16[512,256]{0,1:T(8,128)(2,1)}, bf16[512,256]{0,1:T(8,128)(2,1)S(1)}, u32[]{:S(2)}) copy-start(bf16[512,256]{0,1:T(8,128)(2,1)S(1)} %fusion.31) | copy-start | bytes 786436
  119.7 1.0 copy-start.12
  120.0 6.3 %copy-start.22 = (bf16[512,256]{0,1:T(8,128)(2,1)}, bf16[512,256]{0,1:T(8,128)(2,1)S(1)}, u32[]{:S(2)}) copy-start(bf16[512,256]{0,1:T(8,128)(2,1)S(1)} %fusion.30) | copy-start | bytes 786436
  120.7 1.0 copy-start.9
  121.0 5.6 %copy-start.24 = (bf16[512,256]{0,1:T(8,128)(2,1)}, bf16[512,256]{0,1:T(8,128)(2,1)S(1)}, u32[]{:S(2)}) copy-start(bf16[512,256]{0,1:T(8,128)(2,1)S(1)} %fusion.29) | copy-start | bytes 786436
  121.8 1.0 copy-start.6
  122.1 4.7 %copy-start.26 = (bf16[512,256]{0,1:T(8,128)(2,1)}, bf16[512,256]{0,1:T(8,128)(2,1)S(1)}, u32[]{:S(2)}) copy-start(bf16[512,256]{0,1:T(8,128)(2,1)S(1)} %fusion.28) | copy-start | bytes 786436
  122.8 1.0 copy-start.3
  123.0 4.0 %copy-start.18 = (bf16[512,256]{0,1:T(8,128)(2,1)}, bf16[512,256]{0,1:T(8,128)(2,1)S(1)}, u32[]{:S(2)}) copy-start(bf16[512,256]{0,1:T(8,128)(2,1)S(1)} %fusion.27) | copy-start | bytes 786436
  123.8 0.9 copy-start.31
  124.1 3.1 %copy-start.16 = (bf16[512,256]{0,1:T(8,128)(2,1)}, bf16[512,256]{0,1:T(8,128)(2,1)S(1)}, u32[]{:S(2)}) copy-start(bf16[512,256]{0,1:T(8,128)(2,1)S(1)} %fusion.26) | copy-start | bytes 786436
  125.1 1.0 copy-start.29
  129.1 0.9 copy-start.21
  129.1 1.1 copy-start.23
  129.1 43.9 %all-reduce.5.cloned.1.call-start = ((), (), s32[]{:S(2)}) async-start(), calls=%async_computation.4 | async-start | bytes 262144 | tf_op jit(solution)/shard_map/psum | solution.py:124
  130.2 1.0 copy-start.25
  131.2 0.9 copy-start.27
  132.4 0.7 copy-start.33
  133.1 18.9 %copy-start.34 = (bf16[1,256,512]{1,2,0:T(8,128)(2,1)S(1)}, bf16[1,256,512]{1,2,0:T(8,128)(2,1)}, u32[]{:S(2)}) copy-start(bf16[1,256,512]{1,2,0:T(8,128)(2,1)} %copy-done.33) | copy-start | bytes 786436
  135.1 16.9 %copy-start.19 = (bf16[512,256]{0,1:T(8,128)(2,1)S(1)}, bf16[512,256]{0,1:T(8,128)(2,1)}, u32[]{:S(2)}) copy-start(bf16[512,256]{0,1:T(8,128)(2,1)} %copy-done.18) | copy-start | bytes 786436
  151.9 1.0 copy-start.17
  151.9 31.4 %reduce-scatter.5.cloned.1.call-start = ((), (), s32[]{:S(2)}) async-start(), calls=%async_computation.3 | async-start | bytes 393216 | tf_op jit(solution)/shard_map/reduce_scatter | solution.py:76
Sparse Core Ops, SparseCore 0:
  60.4 55.6 all-reduce.2
  129.2 20.9 reduce-scatter.6
  153.1 19.8 all-reduce.4
  175.6 7.7 reduce-scatter.4
where the time goes:
time: 191 us; the launch traced here: 190 us
  blocking collectives  77.8 us (41%)
  waiting for transfers between devices  42.7 us (22%)
  matrix products  32.4 us (17%)
  local copies, waits for them, and re-layouts  16.6 us (9%)
  between operations  14.8 us (8%)
  other arithmetic  5.53 us (3%)
    all_gather x1, blocking collectives, body(): upstream_all = lax.all_gather(upstream, 'seq', axis=0, tiled=True)  21.1 us
    psum x1, blocking collectives, body(): weighted, totals = lax.psum((partial_sums, partial_totals), 'seq')  19.5 us
    pmax x1, blocking collectives, body(): row_top = lax.pmax(local_top, 'seq')  19.5 us
    psum x1, waiting for transfers between devices, body(): grad_latents = lax.psum(own_grad, 'slide').astype(jnp.float32)  18.5 us
    all_gather x1, blocking collectives, body(): queries = lax.all_gather(latents, 'seq', axis=0, tiled=True)  17.7 us
    unnamed x75, local copies, waits for them, and re-layouts  16.4 us
    unnamed x5, waiting for transfers between devices  15.5 us
    reduce_scatter x1, waiting for transfers between devices, body(): lax.psum_scatter(pooled_part.astype(jnp.bfloat16), 'head', scatter_dimens...  8.71 us
  transfers between devices with their start and end apart: 4, of which 3 were waited for; matrix products, arithmetic and copies ran while one was open for 11% of the time, Pallas kernels for 0%

commit v1 on v0

--- a/solution.py
+++ b/solution.py
@@ -1,16 +1,27 @@
+import functools
+import math
+
 import jax
 import jax.numpy as jnp
 from jax import lax
+from jax.experimental import pallas as pl
+from jax.experimental.pallas import tpu as pltpu
 from jax.sharding import PartitionSpec as P
+
 
 HD = 64
 BLOCK = 128
-
+LANES = 128
+MASK_ROWS = 16
 
 masked_score = -1e30
 
 
-def body(latents, tile_keys, tile_values, tile_mask, latent_counts, out_weight, cotangent):
+bf16 = jnp.bfloat16
+f32 = jnp.float32
+
+
+def gathered_body(latents, tile_keys, tile_values, tile_mask, latent_counts, out_weight, cotangent):
     local_rows = latents.shape[0]
     local_width = latents.shape[1]
     head_count = local_width // HD
@@ -130,6 +141,350 @@
     )
 
 
+def dot_nn(a, b):
+    return lax.dot_general(a, b, (((1,), (0,)), ((), ())), preferred_element_type=f32)
+
+
+def dot_nt(a, b):
+    return lax.dot_general(a, b, (((1,), (1,)), ((), ())), preferred_element_type=f32)
+
+
+def lane_block(index, width):
+    return pl.ds(pl.multiple_of(index * width, width), width)
+
+
+def pack_kernel(n, count_ref, mask_ref, keys_ref, latents_ref, values_ref, weight_ref, cot_ref, *rest):
+    a_outs, v_outs, live_ref = rest[:n], rest[n : 2 * n], rest[2 * n]
+    mask, weight, cot, up_ref, sems = rest[2 * n + 1 :]
+    me = lax.axis_index("seq")
+    tiles, width = v_outs[0].shape
+    rows = cot.shape[0]
+    sources = [
+        (mask_ref, mask),
+        (weight_ref, weight),
+        (cot_ref.at[0], cot),
+    ]
+    for d in range(n):
+        columns = lane_block(lax.rem(me + d, n), width)
+        sources.append((keys_ref.at[0, :, columns], a_outs[d].at[:tiles, :]))
+        sources.append((latents_ref.at[:, columns], a_outs[d].at[tiles : tiles + rows, :]))
+        sources.append((values_ref.at[0, :, columns], v_outs[d]))
+    copies = [
+        pltpu.make_async_copy(source, target, sems.at[i])
+        for i, (source, target) in enumerate(sources)
+    ]
+    for copy in copies:
+        copy.start()
+    for copy in copies[:3]:
+        copy.wait()
+    row_id = lax.broadcasted_iota(jnp.int32, (MASK_ROWS, width), 0)
+    flags = jnp.zeros((MASK_ROWS, width), f32)
+    for block in range(tiles // BLOCK):
+        value = jnp.where(mask[0, block] > 0, 1.0, 0.0)
+        flags = jnp.where(row_id == block, value, flags)
+    lane_row = lax.broadcasted_iota(jnp.int32, (1, rows), 1)
+    projected = dot_nt(weight[...], cot[...])
+    up_ref[...] = jnp.where(lane_row + me * rows < count_ref[0], projected, 0.0).astype(bf16)
+    for d in range(n):
+        owner = lax.rem(me + d, n)
+        a_outs[d][tiles + rows : tiles + rows + width, :] = up_ref[lane_block(owner, width), :]
+        a_outs[d][tiles + rows + width :, :] = flags.astype(bf16)
+        source_row = lane_row + lax.rem(me + n - d, n) * rows
+        live_ref[:, d * rows : (d + 1) * rows] = jnp.where(source_row < count_ref[0], 1.0, 0.0)
+    for copy in copies[3:]:
+        copy.wait()
+
+
+def head_mask(h, shape, axis):
+    return lax.broadcasted_iota(jnp.int32, shape, axis) // HD == h
+
+
+def softmax_kernel(n, heads, rows, *refs):
+    a_refs = refs[:n]
+    expo_ref, total_ref, keys_t_ref, score_ref = refs[n:]
+    width = heads * HD
+    tiles = expo_ref.shape[2]
+    total_rows = n * rows
+    per_block = tiles // BLOCK
+    scale = HD ** (-0.5) * math.log2(math.e)
+    queries = jnp.concatenate([a_refs[d][tiles : tiles + rows, :] for d in range(n)], axis=0)
+    queries_t = queries.astype(f32).T.astype(bf16)
+    valid = []
+    for d in range(n):
+        flags = a_refs[d][tiles + rows + width :, :].astype(f32)
+        for j in range(per_block):
+            valid.append(
+                jnp.concatenate([flags[j : j + 1, :]] * (total_rows // width), axis=1) > 0.5
+            )
+    for h in range(heads):
+        top = jnp.full((1, total_rows), masked_score, f32)
+        query_h = jnp.where(
+            head_mask(h, (width, total_rows), 0), queries_t, jnp.zeros_like(queries_t)
+        )
+        for d in range(n):
+            scored = dot_nn(a_refs[d][:tiles, :], query_h)
+            score_ref[d] = scored
+            for j in range(per_block):
+                block_top = jnp.max(scored[j * BLOCK : (j + 1) * BLOCK], axis=0, keepdims=True)
+                top = jnp.maximum(top, jnp.where(valid[d * per_block + j], block_top, masked_score))
+        total = jnp.zeros((1, total_rows), f32)
+        for d in range(n):
+            for j in range(per_block):
+                part = slice(j * BLOCK, (j + 1) * BLOCK)
+                expos = jnp.where(
+                    valid[d * per_block + j], jnp.exp2((score_ref[d, part, :] - top) * scale), 0.0
+                )
+                total = total + jnp.sum(expos, axis=0, keepdims=True)
+                expo_ref[h, d, part, :] = expos.astype(bf16)
+        total_ref[h] = total
+    for d in range(n):
+        keys_t_ref[d] = a_refs[d][:tiles, :].astype(f32).T.astype(bf16)
+
+
+def value_grads_kernel(n, heads, expo_ref, total_ref, *refs):
+    a_refs, up_ref, outs = refs[:n], refs[n], refs[n + 1 :]
+    factor = HD ** (-0.5)
+    width = heads * HD
+    first = a_refs[0].shape[0] - MASK_ROWS - width
+    upstream_t = jnp.concatenate(
+        [a_refs[d][first : first + width, :] for d in range(n)], axis=1
+    )
+    up_scaled_t = jnp.concatenate(
+        [
+            upstream_t[h * HD : (h + 1) * HD, :].astype(f32) * (factor / total_ref[h])
+            for h in range(heads)
+        ],
+        axis=0,
+    )
+    up_ref[...] = up_scaled_t.astype(bf16)
+    up_scaled = up_scaled_t.T
+    up_heads = [
+        jnp.where(head_mask(h, up_scaled.shape, 1), up_scaled, 0.0).astype(bf16)
+        for h in range(heads)
+    ]
+    for d in range(n):
+        value_grad = dot_nn(expo_ref[0, d], up_heads[0])
+        for h in range(1, heads):
+            value_grad = value_grad + dot_nn(expo_ref[h, d], up_heads[h])
+        outs[d][...] = (value_grad * (1.0 / factor)).astype(bf16)
+
+
+def key_grads_kernel(n, heads, rows, live_ref, expo_ref, total_ref, up_ref, keys_t_ref, *refs):
+    a_refs, v_refs = refs[:n], refs[n : 2 * n]
+    outs, query_grad_ref = refs[2 * n : 3 * n], refs[3 * n]
+    width = heads * HD
+    tiles = v_refs[0].shape[0]
+    total_rows = n * rows
+    live = live_ref[...] > 0.5
+    queries = jnp.concatenate([a_refs[d][tiles : tiles + rows, :] for d in range(n)], axis=0)
+    up_scaled_t = up_ref[...]
+    values_t = [v_refs[d][...].astype(f32).T.astype(bf16) for d in range(n)]
+    attended_list = []
+    delta_list = []
+    for h in range(heads):
+        own_rows = slice(h * HD, (h + 1) * HD)
+        weighted = dot_nn(values_t[0][own_rows, :], expo_ref[h, 0])
+        for d in range(1, n):
+            weighted = weighted + dot_nn(values_t[d][own_rows, :], expo_ref[h, d])
+        attended_h = jnp.where(live, weighted / total_ref[h], 0.0).astype(bf16)
+        delta_list.append(
+            jnp.sum(
+                up_scaled_t[own_rows, :].astype(f32) * attended_h.astype(f32),
+                axis=0,
+                keepdims=True,
+            )
+        )
+        attended_list.append(attended_h)
+    attended = jnp.concatenate(attended_list, axis=0)
+    zero_rows = jnp.zeros_like(queries)
+    zero_cols = jnp.zeros_like(up_scaled_t)
+    query_heads = [jnp.where(head_mask(h, queries.shape, 1), queries, zero_rows) for h in range(heads)]
+    up_heads_t = [
+        jnp.where(head_mask(h, up_scaled_t.shape, 0), up_scaled_t, zero_cols) for h in range(heads)
+    ]
+    query_grad = [jnp.zeros((HD, total_rows), f32) for _ in range(heads)]
+    for d in range(n):
+        key_grad = jnp.zeros((tiles, width), f32)
+        for h in range(heads):
+            grad_prob = dot_nn(v_refs[d][...], up_heads_t[h])
+            grad_score = (expo_ref[h, d].astype(f32) * (grad_prob - delta_list[h])).astype(bf16)
+            key_grad = key_grad + dot_nn(grad_score, query_heads[h])
+            query_grad[h] = query_grad[h] + dot_nn(
+                keys_t_ref[d, h * HD : (h + 1) * HD, :], grad_score
+            )
+        outs[d][:tiles, :] = key_grad.astype(bf16)
+        outs[d][tiles:, :] = attended[:, d * rows : (d + 1) * rows]
+    query_grad_ref[...] = jnp.concatenate(query_grad, axis=0).astype(bf16)
+
+
+def values_home_kernel(n, *refs):
+    c_refs, value_grad_ref = refs[:n], refs[n]
+    me = lax.axis_index("seq")
+    width = c_refs[0].shape[1]
+    for d in range(n):
+        value_grad_ref[0, :, lane_block(lax.rem(me + d, n), width)] = c_refs[d][...]
+
+
+def pool_kernel(n, weight_ref, *refs):
+    k_refs = refs[:n]
+    key_grad_ref, kept_ref, sent_ref = refs[n : n + 3]
+    me, side = lax.axis_index("seq"), lax.axis_index("head")
+    width = k_refs[0].shape[1]
+    tiles = key_grad_ref.shape[1]
+    half = kept_ref.shape[1]
+    kept = jnp.zeros(kept_ref.shape, f32)
+    sent = jnp.zeros(sent_ref.shape, f32)
+    for d in range(n):
+        owner = lax.rem(me + d, n)
+        key_grad_ref[0, :, lane_block(owner, width)] = k_refs[d][:tiles, :]
+        attended = k_refs[d][tiles:, :].astype(f32).T.astype(bf16)
+        inputs = lane_block(owner, width)
+        kept = kept + dot_nn(attended, weight_ref[inputs, lane_block(side, half)])
+        sent = sent + dot_nn(attended, weight_ref[inputs, lane_block(1 - side, half)])
+    kept_ref[...] = kept
+    sent_ref[...] = sent.astype(bf16)
+
+
+def join_kernel(n, own_ref, other_ref, *outs):
+    rows = outs[0].shape[1]
+    both = (own_ref[...].astype(f32) + other_ref[...].astype(f32)).astype(bf16)
+    for d in range(n):
+        outs[d][...] = both[:, d * rows : (d + 1) * rows]
+
+
+def last_kernel(n, kept_ref, came_ref, *refs):
+    g_refs, latent_grad_ref, pooled_ref = refs[:n], refs[n], refs[n + 1]
+    me = lax.axis_index("seq")
+    width = g_refs[0].shape[0]
+    for d in range(n):
+        columns = lane_block(lax.rem(me + d, n), width)
+        latent_grad_ref[:, columns] = g_refs[d][...].astype(f32).T
+    pooled_ref[0] = (kept_ref[...] + came_ref[...].astype(f32)).astype(bf16)
+
+
+SMEM = pl.BlockSpec(memory_space=pltpu.SMEM)
+HBM = pl.BlockSpec(memory_space=pltpu.HBM)
+VMEM = pl.BlockSpec(memory_space=pltpu.VMEM)
+
+
+def call(kernel, out_shape, operands, flops, scratch=(), grant=8, spaces=None):
+    moved = sum(x.size * x.dtype.itemsize for x in operands)
+    moved += sum(math.prod(x.shape) * x.dtype.itemsize for x in out_shape)
+    return pl.pallas_call(
+        kernel,
+        out_shape=out_shape,
+        in_specs=spaces or [VMEM] * len(operands),
+        out_specs=[VMEM] * len(out_shape),
+        scratch_shapes=list(scratch),
+        cost_estimate=pl.CostEstimate(flops=int(flops), bytes_accessed=moved, transcendentals=0),
+        compiler_params=pltpu.CompilerParams(vmem_limit_bytes=grant * 1024 * 1024),
+    )(*operands)
+
+
+def exchanged_body(n, sides, latents, tile_keys, tile_values, tile_mask, latent_counts, out_weight, cotangent):
+    rows, local_width = latents.shape
+    tiles = tile_keys.shape[1]
+    out_width = out_weight.shape[1]
+    heads = local_width // HD // n
+    width = heads * HD
+    total_rows = n * rows
+    sds = jax.ShapeDtypeStruct
+    product = 2 * total_rows * n * tiles * width
+
+    def spread(pieces, sign):
+        return [pieces[0]] + [
+            lax.ppermute(pieces[d], "seq", [(i, (i + sign * d) % n) for i in range(n)])
+            for d in range(1, n)
+        ]
+
+    *packed, live = call(
+        functools.partial(pack_kernel, n),
+        [sds((tiles + rows + width + MASK_ROWS, width), bf16)] * n
+        + [sds((tiles, width), bf16)] * n
+        + [sds((1, total_rows), f32)],
+        (
+            latent_counts,
+            *(
+                pltpu.with_memory_space_constraint(x, pltpu.HBM)
+                for x in (tile_mask, tile_keys, latents, tile_values, out_weight, cotangent)
+            ),
+        ),
+        2 * rows * local_width * out_width,
+        [
+            pltpu.SMEM(tile_mask.shape, jnp.int32),
+            pltpu.VMEM(out_weight.shape, bf16),
+            pltpu.VMEM(cotangent.shape[1:], bf16),
+            pltpu.VMEM((local_width, rows), bf16),
+            pltpu.SemaphoreType.DMA((3 + 3 * n,)),
+        ],
+        spaces=[SMEM] + [HBM] * 6,
+    )
+    a_list = spread(packed[:n], 1)
+    v_list = spread(packed[n:], 1)
+    expos, totals, keys_t = call(
+        functools.partial(softmax_kernel, n, heads, rows),
+        [
+            sds((heads, n, tiles, total_rows), bf16),
+            sds((heads, 1, total_rows), f32),
+            sds((n, width, tiles), bf16),
+        ],
+        a_list,
+        product,
+        [pltpu.VMEM((n, tiles, total_rows), f32)],
+        16,
+    )
+    up_scaled, *c_out = call(
+        functools.partial(value_grads_kernel, n, heads),
+        [sds((width, total_rows), bf16)] + [sds((tiles, width), bf16)] * n,
+        (expos, totals, *a_list),
+        product,
+        (),
+        16,
+    )
+    c_list = spread(c_out, -1)
+    *k_out, query_grad = call(
+        functools.partial(key_grads_kernel, n, heads, rows),
+        [sds((tiles + width, width), bf16)] * n + [sds((width, total_rows), bf16)],
+        (live, expos, totals, up_scaled, keys_t, *a_list, *v_list),
+        4 * product,
+        (),
+        16,
+    )
+    other_sum = None
+    for step in range(1, sides):
+        came = lax.ppermute(query_grad, "slide", [(i, (i + step) % sides) for i in range(sides)])
+        other_sum = came if other_sum is None else other_sum.astype(f32) + came.astype(f32)
+    k_list = spread(k_out, -1)
+    joined = call(
+        functools.partial(join_kernel, n),
+        [sds((width, rows), bf16)] * n,
+        (query_grad, other_sum),
+        1e6,
+    )
+    g_list = spread(joined, -1)
+    (value_grads,) = call(
+        functools.partial(values_home_kernel, n), [sds(tile_values.shape, bf16)], c_list, 1e6
+    )
+    key_grads, kept, sent = call(
+        functools.partial(pool_kernel, n),
+        [
+            sds(tile_keys.shape, bf16),
+            sds((rows, out_width // 2), f32),
+            sds((rows, out_width // 2), bf16),
+        ],
+        (out_weight, *k_list),
+        2 * rows * local_width * out_width,
+    )
+    came = lax.ppermute(sent, "head", [(0, 1), (1, 0)])
+    latent_grads, pooled = call(
+        functools.partial(last_kernel, n),
+        [sds(latents.shape, f32), sds((1, rows, out_width // 2), bf16)],
+        (kept, came, *g_list),
+        1e6,
+    )
+    return pooled, latent_grads, key_grads, value_grads
+
+
 def solution(mesh):
     placed = (
         P(("groups", "seq"), "head"),
@@ -140,6 +495,23 @@
         P("head", None),
         P(("groups", "slide"), "seq", None),
     )
+    n, sides = mesh.shape["seq"], mesh.shape["slide"]
+
+    def body(latents, tile_keys, *rest):
+        rows, local_width = latents.shape
+        tiles = tile_keys.shape[1]
+        fits = (
+            mesh.shape["head"] == 2
+            and sides > 1
+            and local_width % (n * LANES) == 0
+            and local_width // n == rows
+            and tiles % BLOCK == 0
+            and tiles // BLOCK <= MASK_ROWS
+        )
+        if fits:
+            return exchanged_body(n, sides, latents, tile_keys, *rest)
+        return gathered_body(latents, tile_keys, *rest)
+
     return jax.shard_map(
         body,
         mesh=mesh,

time: 191 us -> 56.8 us (0.30)
  blocking collectives: 77.8 us -> 0 us
  matrix products: 32.4 us -> 0 us
  starting transfers between devices: 0.16 us -> 20.8 us
  waiting for transfers between devices: 42.7 us -> 24.8 us
  local copies, waits for them, and re-layouts: 16.6 us -> 0.01 us
  between operations: 14.8 us -> 1.34 us
  Pallas kernels: 0 us -> 9.66 us
  other arithmetic: 5.53 us -> 0 us
    all_gather x2 -> x0, blocking collectives: 38.8 us -> none  [the longest x1 21.1 us: body(): upstream_all = lax.all_gather(upstream, 'seq', axis=0, tiled=True)]
    dot_general x50 -> x0, matrix products: 32.4 us -> none  [the longest x8 8.47 us: body(): jnp.dot(expos.astype(jnp.bfloat16), value_block[:, columns], preferred_el...]
    ppermute x0 -> x17, waiting for transfers between devices: none -> 24.8 us  [the longest x15 24.8 us: spread(): lax.ppermute(pieces[d], 'seq', [(i, (i + sign * d) % n) for i in range(n)])]
    ppermute x0 -> x17, starting transfers between devices: none -> 20.8 us  [the longest x15 19.3 us: spread(): lax.ppermute(pieces[d], 'seq', [(i, (i + sign * d) % n) for i in range(n)])]
    psum x1 -> x0, blocking collectives: 19.5 us -> none  [body(): weighted, totals = lax.psum((partial_sums, partial_totals), 'seq')]
    pmax x1 -> x0, blocking collectives: 19.5 us -> none  [body(): row_top = lax.pmax(local_top, 'seq')]
    psum x2 -> x0, waiting for transfers between devices: 18.5 us -> none  [the longest x1 18.5 us: body(): grad_latents = lax.psum(own_grad, 'slide').astype(jnp.float32)]
    unnamed x75 -> x2, local copies, waits for them, and re-layouts: 16.4 us -> 0.01 us
  transfers between devices with their start and end apart: 4 -> 17, of which waited for: 3 -> 10; matrix products, arithmetic and copies ran while one was open for 11% -> 0% of each run, Pallas kernels for 0% -> 8%
where the time goes in v1:
time: 56.8 us; the launch traced here: 56.6 us
  waiting for transfers between devices  24.8 us (44%)
  starting transfers between devices  20.8 us (37%)
  Pallas kernels  9.66 us (17%)
  between operations  1.34 us (2%)
    ppermute x15, waiting for transfers between devices, spread(): lax.ppermute(pieces[d], 'seq', [(i, (i + sign * d) % n) for i in range(n)])  24.8 us
    ppermute x15, starting transfers between devices, spread(): lax.ppermute(pieces[d], 'seq', [(i, (i + sign * d) % n) for i in range(n)])  19.3 us
    pallas_call x8, Pallas kernels, call(): pl.pallas_call(kernel, out_shape=out_shape, in_specs=spaces or [VMEM] * l...  9.66 us
    ppermute x1, starting transfers between devices, exchanged_body(): lax.ppermute(query_grad, 'slide', [(i, (i + step) % sides) for i in range...  1.5 us
  transfers between devices with their start and end apart: 17, of which 10 were waited for; matrix products, arithmetic and copies ran while one was open for 0% of the time, Pallas kernels for 8%

profile of v1, /device:TPU:0, one launch (start us, length us, event | category | flops | bytes accessed | tf_op | source)
XLA Modules:
  0.0 56.6 jit_solution(4328907114868529154)
XLA Ops:
  1.3 1.9 %shard_map.102 = (bf16[528,128]{1,0:T(8,128)(2,1)S(1)}, bf16[528,128]{1,0:T(8,128)(2,1)S(1)}, bf16[528,128]{1,0:T(8,128)(2,1)S(1)}, bf16[528,128]{1,0:T(8,128)(2...) custom-call(s32[1]{0:T(128)S(6)} %copy.11.count_ref, ...), custom_call_target="tpu_custom_call" | custom-call | flops 134217728 | bytes 2770956 | tf_op jit(solution)/shard_map/pallas_call | solution.py:373
  3.2 3.1 %collective-permute-start = (bf16[528,128]{1,0:T(8,128)(2,1)S(1)}, bf16[528,128]{1,0:T(8,128)(2,1)S(1)}, u32[]{:S(2)}, u32[]{:S(2)}) collective-permute-start(bf16[528,128]{1,0:T(8,128)(2,1)S(1)} %get-tuple-element.37), channel_id=1, source_target_pairs={{0,4},{4,8},{8,12},{12,0},{1,5},{5,9},{9,13},{13,1},{2,6},{6,10},{... | collective-permute-start | bytes 405512 | tf_op jit(solution)/shard_map/ppermute | solution.py:396
  6.3 2.6 %collective-permute-start.1 = (bf16[528,128]{1,0:T(8,128)(2,1)S(1)}, bf16[528,128]{1,0:T(8,128)(2,1)S(1)}, u32[]{:S(2)}, u32[]{:S(2)}) collective-permute-start(bf16[528,128]{1,0:T(8,128)(2,1)S(1)} %get-tuple-element.38), channel_id=1, source_target_pairs={{0,8},{4,12},{8,0},{12,4},{1,9},{5,13},{9,1},{13,5},{2,10},{6,14},... | collective-permute-start | bytes 405512 | tf_op jit(solution)/shard_map/ppermute | solution.py:396
  8.9 1.3 %collective-permute-start.2 = (bf16[528,128]{1,0:T(8,128)(2,1)S(1)}, bf16[528,128]{1,0:T(8,128)(2,1)S(1)}, u32[]{:S(2)}, u32[]{:S(2)}) collective-permute-start(bf16[528,128]{1,0:T(8,128)(2,1)S(1)} %get-tuple-element.39), channel_id=1, source_target_pairs={{0,12},{4,0},{8,4},{12,8},{1,13},{5,1},{9,5},{13,9},{2,14},{6,2},{... | collective-permute-start | bytes 405512 | tf_op jit(solution)/shard_map/ppermute | solution.py:396
  10.2 0.7 %collective-permute-start.3 = (bf16[256,128]{1,0:T(8,128)(2,1)S(1)}, bf16[256,128]{1,0:T(8,128)(2,1)S(1)}, u32[]{:S(2)}, u32[]{:S(2)}) collective-permute-start(bf16[256,128]{1,0:T(8,128)(2,1)S(1)} %get-tuple-element.45), channel_id=1, source_target_pairs={{0,4},{4,8},{8,12},{12,0},{1,5},{5,9},{9,13},{13,1},{2,6},{6,10},{... | collective-permute-start | bytes 196616 | tf_op jit(solution)/shard_map/ppermute | solution.py:396
  10.9 0.3 collective-permute-start.4
  11.2 1.6 %collective-permute-done.refs_1_ = bf16[528,128]{1,0:T(8,128)(2,1)S(1)} collective-permute-done((bf16[528,128]{1,0:T(8,128)(2,1)S(1)}, bf16[528,128]{1,0:T(8,128)(2,1)S(1)}, u32[]{:S(2)}, u32[]{:S(2)}) %collective-permute-start) | collective-permute-done | bytes 135200 | tf_op jit(solution)/shard_map/ppermute | solution.py:396
  12.8 2.1 %collective-permute-start.5 = (bf16[256,128]{1,0:T(8,128)(2,1)S(1)}, bf16[256,128]{1,0:T(8,128)(2,1)S(1)}, u32[]{:S(2)}, u32[]{:S(2)}) collective-permute-start(bf16[256,128]{1,0:T(8,128)(2,1)S(1)} %get-tuple-element.47), channel_id=1, source_target_pairs={{0,12},{4,0},{8,4},{12,8},{1,13},{5,1},{9,5},{13,9},{2,14},{6,2},{... | collective-permute-start | bytes 196616 | tf_op jit(solution)/shard_map/ppermute | solution.py:396
  14.9 3.8 %collective-permute-done.1.refs_2_ = bf16[528,128]{1,0:T(8,128)(2,1)S(1)} collective-permute-done((bf16[528,128]{1,0:T(8,128)(2,1)S(1)}, bf16[528,128]{1,0:T(8,128)(2,1)S(1)}, u32[]{:S(2)}, u32[]{:S(2)}) %collective-permute-start.1) | collective-permute-done | bytes 135200 | tf_op jit(solution)/shard_map/ppermute | solution.py:396
  18.7 0.7 %collective-permute-done.2.refs_3_ = bf16[528,128]{1,0:T(8,128)(2,1)S(1)} collective-permute-done((bf16[528,128]{1,0:T(8,128)(2,1)S(1)}, bf16[528,128]{1,0:T(8,128)(2,1)S(1)}, u32[]{:S(2)}, u32[]{:S(2)}) %collective-permute-start.2) | collective-permute-done | bytes 135200 | tf_op jit(solution)/shard_map/ppermute | solution.py:396
  19.4 1.6 %shard_map.103 = (bf16[2,4,256,512]{3,2,1,0:T(8,128)(2,1)S(1)}, f32[2,1,512]{2,1,0:T(1,128)S(1)}, bf16[4,128,256]{2,1,0:T(8,128)(2,1)S(1)}) custom-call(bf16[528,128]{1,0:T(8,128)(2,1)S(1)} %get-tuple-element.36.refs_0_, bf16[528,128]{1,0:T(8,128)(2,1)S(1)} %collective-permute-done.refs_1_, bf16[528,128]{1,0:T(8,128)(2,1)S(1)} %collective-permute-done.1.refs_2_, ...), custom_call_target="tpu_custom_call" | custom-call | flops 134217728 | bytes 2904064 | tf_op jit(solution)/shard_map/pallas_call | solution.py:373
  21.0 0.8 %shard_map.104 = (bf16[128,512]{1,0:T(8,128)(2,1)S(1)}, bf16[256,128]{1,0:T(8,128)(2,1)S(1)}, bf16[256,128]{1,0:T(8,128)(2,1)S(1)}, bf16[256,128]{1,0:T(8,128)(2,1)S(1)}, bf16[256,128]{1,0:T(8,128)(2,1)S(1)}) custom-call(bf16[2,4,256,512]{3,2,1,0:T(8,128)(2,1)S(1)} %get-tuple-element.40.expo_ref, f32[2,1,512]{2,1,0:T(1,128)S(1)} %get-tuple-element.41.total_ref, ...), custom_call_target="tpu_custom_call" | custom-call | flops 134217728 | bytes 3035136 | tf_op jit(solution)/shard_map/pallas_call | solution.py:373
  21.8 0.0 copy-start
  21.8 0.0 collective-permute-done.3.refs_5_
  21.8 3.1 %collective-permute-done.4.refs_6_ = bf16[256,128]{1,0:T(8,128)(2,1)S(1)} collective-permute-done((bf16[256,128]{1,0:T(8,128)(2,1)S(1)}, bf16[256,128]{1,0:T(8,128)(2,1)S(1)}, u32[]{:S(2)}, u32[]{:S(2)}) %collective-permute-start.4) | collective-permute-done | bytes 65568 | tf_op jit(solution)/shard_map/ppermute | solution.py:396
  24.9 0.0 collective-permute-done.5.refs_7_
  24.9 2.6 %shard_map.105 = (bf16[384,128]{1,0:T(8,128)(2,1)S(1)}, bf16[384,128]{1,0:T(8,128)(2,1)S(1)}, bf16[384,128]{1,0:T(8,128)(2,1)S(1)}, bf16[384,128]{1,0:T(8,128)(2,1)S(1)}, bf16[128,512]{1,0:T(8,128)(2,1)S(1)}) custom-call(f32[1,512]{1,0:T(1,128)S(1)} %get-tuple-element.35.live_ref, bf16[2,4,256,512]{3,2,1,0:T(8,128)(2,1)S(1)} %get-tuple-element.40.expo_ref, ...), custom_call_target="tpu_custom_call" | custom-call | flops 536870912 | bytes 3823616 | tf_op jit(solution)/shard_map/pallas_call | solution.py:373
  27.5 3.7 %collective-permute-start.6 = (bf16[384,128]{1,0:T(8,128)(2,1)S(1)}, bf16[384,128]{1,0:T(8,128)(2,1)S(1)}, u32[]{:S(2)}, u32[]{:S(2)}) collective-permute-start(bf16[384,128]{1,0:T(8,128)(2,1)S(1)} %get-tuple-element.49), channel_id=1, source_target_pairs={{0,12},{4,0},{8,4},{12,8},{1,13},{5,1},{9,5},{13,9},{2,14},{6,2},{... | collective-permute-start | bytes 294920 | tf_op jit(solution)/shard_map/ppermute | solution.py:396
  31.3 0.0 collective-permute-start.7
  31.3 0.6 %collective-permute-start.8 = (bf16[384,128]{1,0:T(8,128)(2,1)S(1)}, bf16[384,128]{1,0:T(8,128)(2,1)S(1)}, u32[]{:S(2)}, u32[]{:S(2)}) collective-permute-start(bf16[384,128]{1,0:T(8,128)(2,1)S(1)} %get-tuple-element.51), channel_id=1, source_target_pairs={{0,4},{4,8},{8,12},{12,0},{1,5},{5,9},{9,13},{13,1},{2,6},{6,10},{... | collective-permute-start | bytes 294920 | tf_op jit(solution)/shard_map/ppermute | solution.py:396
  31.9 1.5 %collective-permute-start.10 = (bf16[128,512]{1,0:T(8,128)(2,1)S(1)}, bf16[128,512]{1,0:T(8,128)(2,1)S(1)}, u32[]{:S(2)}, u32[]{:S(2)}) collective-permute-start(bf16[128,512]{1,0:T(8,128)(2,1)S(1)} %get-tuple-element.54.own_ref), channel_id=1, source_target_pairs={{0,2},{2,0},{1,3},{3,1},{4,6},{6,4},{5,7},{7,5},{8,10},{10,8},{9,1... | collective-permute-start | bytes 393224 | tf_op jit(solution)/shard_map/ppermute | solution.py:455
  33.4 0.5 collective-permute-done.6.refs_1_
  33.9 6.0 %collective-permute-done.7.refs_2_ = bf16[384,128]{1,0:T(8,128)(2,1)S(1)} collective-permute-done((bf16[384,128]{1,0:T(8,128)(2,1)S(1)}, bf16[384,128]{1,0:T(8,128)(2,1)S(1)}, u32[]{:S(2)}, u32[]{:S(2)}) %collective-permute-start.7) | collective-permute-done | bytes 98336 | tf_op jit(solution)/shard_map/ppermute | solution.py:396
  39.9 0.0 collective-permute-done.8.refs_3_
  39.9 0.0 copy-done
  39.9 1.1 %shard_map.106 = (bf16[1,256,512]{2,1,0:T(8,128)(2,1)}, f32[128,512]{1,0:T(8,128)S(1)}, bf16[128,512]{1,0:T(8,128)(2,1)S(1)}) custom-call(bf16[512,1024]{1,0:T(8,128)(2,1)S(1)} %copy-done, bf16[384,128]{1,0:T(8,128)(2,1)S(1)} %get-tuple-element.48.refs_0_, bf16[384,128]{1,0:T(8,128)(2,1)S(1)} %collective-permute-done.6.refs_1_, ...), custom_call_target="tpu_custom_call" | custom-call | flops 134217728 | bytes 2097152 | tf_op jit(solution)/shard_map/pallas_call | solution.py:373
  41.1 0.0 collective-permute-start.9
  41.1 0.4 collective-permute-start.14
  41.5 0.5 collective-permute-start.15
  42.0 1.9 %collective-permute-start.16 = (bf16[256,128]{1,0:T(8,128)(2,1)S(1)}, bf16[256,128]{1,0:T(8,128)(2,1)S(1)}, u32[]{:S(2)}, u32[]{:S(2)}) collective-permute-start(bf16[256,128]{1,0:T(8,128)(2,1)S(1)} %get-tuple-element.65), channel_id=1, source_target_pairs={{0,4},{4,8},{8,12},{12,0},{1,5},{5,9},{9,13},{13,1},{2,6},{6,10},{... | collective-permute-start | bytes 196616 | tf_op jit(solution)/shard_map/ppermute | solution.py:396
  43.8 0.0 collective-permute-done.10.other_ref
  43.9 2.0 %collective-permute-start.11 = (bf16[128,128]{1,0:T(8,128)(2,1)S(1)}, bf16[128,128]{1,0:T(8,128)(2,1)S(1)}, u32[]{:S(2)}, u32[]{:S(2)}) collective-permute-start(bf16[128,128]{1,0:T(8,128)(2,1)S(1)} %get-tuple-element.56), channel_id=1, source_target_pairs={{0,12},{4,0},{8,4},{12,8},{1,13},{5,1},{9,5},{13,9},{2,14},{6,2},{... | collective-permute-start | bytes 98312 | tf_op jit(solution)/shard_map/ppermute | solution.py:396
  45.9 1.1 %collective-permute-done.14.refs_1_ = bf16[256,128]{1,0:T(8,128)(2,1)S(1)} collective-permute-done((bf16[256,128]{1,0:T(8,128)(2,1)S(1)}, bf16[256,128]{1,0:T(8,128)(2,1)S(1)}, u32[]{:S(2)}, u32[]{:S(2)}) %collective-permute-start.14) | collective-permute-done | bytes 65568 | tf_op jit(solution)/shard_map/ppermute | solution.py:396
  47.0 0.0 collective-permute-start.12
  47.0 3.1 %collective-permute-done.15.refs_2_ = bf16[256,128]{1,0:T(8,128)(2,1)S(1)} collective-permute-done((bf16[256,128]{1,0:T(8,128)(2,1)S(1)}, bf16[256,128]{1,0:T(8,128)(2,1)S(1)}, u32[]{:S(2)}, u32[]{:S(2)}) %collective-permute-start.15) | collective-permute-done | bytes 65568 | tf_op jit(solution)/shard_map/ppermute | solution.py:396
  50.1 0.0 collective-permute-start.13
  50.1 0.0 collective-permute-done.16.refs_3_
  50.1 0.8 %shard_map.109 = bf16[1,256,512]{2,1,0:T(8,128)(2,1)} custom-call(bf16[256,128]{1,0:T(8,128)(2,1)S(1)} %get-tuple-element.62.refs_0_, bf16[256,128]{1,0:T(8,128)(2,1)S(1)} %collective-permute-done.14.refs_1_, bf16[256,128]{1,0:T(8,128)(2,1)S(1)} %collective-permute-done.15.refs_2_, bf16[256,128]{1,0:T(8,128)(2,1)S(1)} %collective-permute-done.16.refs_3_), custom_call_target="tpu_custom_call" | custom-call | flops 1000000 | bytes 524288 | tf_op jit(solution)/shard_map/pallas_call | solution.py:373
  50.9 0.0 collective-permute-done.11.refs_1_
  50.9 0.9 %collective-permute-done.12.refs_2_ = bf16[128,128]{1,0:T(8,128)(2,1)S(1)} collective-permute-done((bf16[128,128]{1,0:T(8,128)(2,1)S(1)}, bf16[128,128]{1,0:T(8,128)(2,1)S(1)}, u32[]{:S(2)}, u32[]{:S(2)}) %collective-permute-start.12) | collective-permute-done | bytes 32800 | tf_op jit(solution)/shard_map/ppermute | solution.py:396
  51.8 4.0 %collective-permute-done.13.refs_3_ = bf16[128,128]{1,0:T(8,128)(2,1)S(1)} collective-permute-done((bf16[128,128]{1,0:T(8,128)(2,1)S(1)}, bf16[128,128]{1,0:T(8,128)(2,1)S(1)}, u32[]{:S(2)}, u32[]{:S(2)}) %collective-permute-start.13) | collective-permute-done | bytes 32800 | tf_op jit(solution)/shard_map/ppermute | solution.py:396
  55.8 0.0 collective-permute-done.9.came_ref
  55.8 0.8 %shard_map.108 = (f32[128,512]{1,0:T(8,128)}, bf16[1,128,512]{2,1,0:T(8,128)(2,1)}) custom-call(f32[128,512]{1,0:T(8,128)S(1)} %get-tuple-element.52.kept_ref, bf16[128,512]{1,0:T(8,128)(2,1)S(1)} %collective-permute-done.9.came_ref, bf16[128,128]{1,0:T(8,128)(2,1)S(1)} %get-tuple-element.55.refs_0_, bf16[128,128]{1,0:T(8,128)(2,1)S(1)} %collective-permute-done.11.refs_1_, ...), custom_call_target="tpu_custom_call" | custom-call | flops 1000000 | bytes 917504 | tf_op jit(solution)/shard_map/pallas_call | solution.py:373
  (1 shorter events, 0.0 us)
Async XLA Ops:
  3.2 9.7 %collective-permute-start = (bf16[528,128]{1,0:T(8,128)(2,1)S(1)}, bf16[528,128]{1,0:T(8,128)(2,1)S(1)}, u32[]{:S(2)}, u32[]{:S(2)}) collective-permute-start(bf16[528,128]{1,0:T(8,128)(2,1)S(1)} %get-tuple-element.37), channel_id=1, source_target_pairs={{0,4},{4,8},{8,12},{12,0},{1,5},{5,9},{9,13},{13,1},{2,6},{6,10},{... | collective-permute-start | bytes 405512 | tf_op jit(solution)/shard_map/ppermute | solution.py:396
  6.3 12.4 %collective-permute-start.1 = (bf16[528,128]{1,0:T(8,128)(2,1)S(1)}, bf16[528,128]{1,0:T(8,128)(2,1)S(1)}, u32[]{:S(2)}, u32[]{:S(2)}) collective-permute-start(bf16[528,128]{1,0:T(8,128)(2,1)S(1)} %get-tuple-element.38), channel_id=1, source_target_pairs={{0,8},{4,12},{8,0},{12,4},{1,9},{5,13},{9,1},{13,5},{2,10},{6,14},... | collective-permute-start | bytes 405512 | tf_op jit(solution)/shard_map/ppermute | solution.py:396
  8.9 10.5 %collective-permute-start.2 = (bf16[528,128]{1,0:T(8,128)(2,1)S(1)}, bf16[528,128]{1,0:T(8,128)(2,1)S(1)}, u32[]{:S(2)}, u32[]{:S(2)}) collective-permute-start(bf16[528,128]{1,0:T(8,128)(2,1)S(1)} %get-tuple-element.39), channel_id=1, source_target_pairs={{0,12},{4,0},{8,4},{12,8},{1,13},{5,1},{9,5},{13,9},{2,14},{6,2},{... | collective-permute-start | bytes 405512 | tf_op jit(solution)/shard_map/ppermute | solution.py:396
  10.2 11.6 %collective-permute-start.3 = (bf16[256,128]{1,0:T(8,128)(2,1)S(1)}, bf16[256,128]{1,0:T(8,128)(2,1)S(1)}, u32[]{:S(2)}, u32[]{:S(2)}) collective-permute-start(bf16[256,128]{1,0:T(8,128)(2,1)S(1)} %get-tuple-element.45), channel_id=1, source_target_pairs={{0,4},{4,8},{8,12},{12,0},{1,5},{5,9},{9,13},{13,1},{2,6},{6,10},{... | collective-permute-start | bytes 196616 | tf_op jit(solution)/shard_map/ppermute | solution.py:396
  10.9 14.0 %collective-permute-start.4 = (bf16[256,128]{1,0:T(8,128)(2,1)S(1)}, bf16[256,128]{1,0:T(8,128)(2,1)S(1)}, u32[]{:S(2)}, u32[]{:S(2)}) collective-permute-start(bf16[256,128]{1,0:T(8,128)(2,1)S(1)} %get-tuple-element.46), channel_id=1, source_target_pairs={{0,8},{4,12},{8,0},{12,4},{1,9},{5,13},{9,1},{13,5},{2,10},{6,14},... | collective-permute-start | bytes 196616 | tf_op jit(solution)/shard_map/ppermute | solution.py:396
  12.8 12.1 %collective-permute-start.5 = (bf16[256,128]{1,0:T(8,128)(2,1)S(1)}, bf16[256,128]{1,0:T(8,128)(2,1)S(1)}, u32[]{:S(2)}, u32[]{:S(2)}) collective-permute-start(bf16[256,128]{1,0:T(8,128)(2,1)S(1)} %get-tuple-element.47), channel_id=1, source_target_pairs={{0,12},{4,0},{8,4},{12,8},{1,13},{5,1},{9,5},{13,9},{2,14},{6,2},{... | collective-permute-start | bytes 196616 | tf_op jit(solution)/shard_map/ppermute | solution.py:396
  21.8 18.1 %copy-start = (bf16[512,1024]{1,0:T(8,128)(2,1)S(1)}, bf16[512,1024]{1,0:T(8,128)(2,1)}, u32[]{:S(2)}) copy-start(bf16[512,1024]{1,0:T(8,128)(2,1)} %weight_ref.3) | copy-start | bytes 3145732
  27.5 6.4 %collective-permute-start.6 = (bf16[384,128]{1,0:T(8,128)(2,1)S(1)}, bf16[384,128]{1,0:T(8,128)(2,1)S(1)}, u32[]{:S(2)}, u32[]{:S(2)}) collective-permute-start(bf16[384,128]{1,0:T(8,128)(2,1)S(1)} %get-tuple-element.49), channel_id=1, source_target_pairs={{0,12},{4,0},{8,4},{12,8},{1,13},{5,1},{9,5},{13,9},{2,14},{6,2},{... | collective-permute-start | bytes 294920 | tf_op jit(solution)/shard_map/ppermute | solution.py:396
  31.3 8.7 %collective-permute-start.7 = (bf16[384,128]{1,0:T(8,128)(2,1)S(1)}, bf16[384,128]{1,0:T(8,128)(2,1)S(1)}, u32[]{:S(2)}, u32[]{:S(2)}) collective-permute-start(bf16[384,128]{1,0:T(8,128)(2,1)S(1)} %get-tuple-element.50), channel_id=1, source_target_pairs={{0,8},{4,12},{8,0},{12,4},{1,9},{5,13},{9,1},{13,5},{2,10},{6,14},... | collective-permute-start | bytes 294920 | tf_op jit(solution)/shard_map/ppermute | solution.py:396
  31.3 8.7 %collective-permute-start.8 = (bf16[384,128]{1,0:T(8,128)(2,1)S(1)}, bf16[384,128]{1,0:T(8,128)(2,1)S(1)}, u32[]{:S(2)}, u32[]{:S(2)}) collective-permute-start(bf16[384,128]{1,0:T(8,128)(2,1)S(1)} %get-tuple-element.51), channel_id=1, source_target_pairs={{0,4},{4,8},{8,12},{12,0},{1,5},{5,9},{9,13},{13,1},{2,6},{6,10},{... | collective-permute-start | bytes 294920 | tf_op jit(solution)/shard_map/ppermute | solution.py:396
  31.9 11.9 %collective-permute-start.10 = (bf16[128,512]{1,0:T(8,128)(2,1)S(1)}, bf16[128,512]{1,0:T(8,128)(2,1)S(1)}, u32[]{:S(2)}, u32[]{:S(2)}) collective-permute-start(bf16[128,512]{1,0:T(8,128)(2,1)S(1)} %get-tuple-element.54.own_ref), channel_id=1, source_target_pairs={{0,2},{2,0},{1,3},{3,1},{4,6},{6,4},{5,7},{7,5},{8,10},{10,8},{9,1... | collective-permute-start | bytes 393224 | tf_op jit(solution)/shard_map/ppermute | solution.py:455
  41.1 14.7 %collective-permute-start.9 = (bf16[128,512]{1,0:T(8,128)(2,1)S(1)}, bf16[128,512]{1,0:T(8,128)(2,1)S(1)}, u32[]{:S(2)}, u32[]{:S(2)}) collective-permute-start(bf16[128,512]{1,0:T(8,128)(2,1)S(1)} %get-tuple-element.53), channel_id=1, source_target_pairs={{0,1},{1,0},{2,3},{3,2},{4,5},{5,4},{6,7},{7,6},{8,9},{9,8},{10,11... | collective-permute-start | bytes 393224 | tf_op jit(solution)/shard_map/ppermute | solution.py:478
  41.1 5.9 %collective-permute-start.14 = (bf16[256,128]{1,0:T(8,128)(2,1)S(1)}, bf16[256,128]{1,0:T(8,128)(2,1)S(1)}, u32[]{:S(2)}, u32[]{:S(2)}) collective-permute-start(bf16[256,128]{1,0:T(8,128)(2,1)S(1)} %get-tuple-element.63), channel_id=1, source_target_pairs={{0,12},{4,0},{8,4},{12,8},{1,13},{5,1},{9,5},{13,9},{2,14},{6,2},{... | collective-permute-start | bytes 196616 | tf_op jit(solution)/shard_map/ppermute | solution.py:396
  41.5 8.6 %collective-permute-start.15 = (bf16[256,128]{1,0:T(8,128)(2,1)S(1)}, bf16[256,128]{1,0:T(8,128)(2,1)S(1)}, u32[]{:S(2)}, u32[]{:S(2)}) collective-permute-start(bf16[256,128]{1,0:T(8,128)(2,1)S(1)} %get-tuple-element.64), channel_id=1, source_target_pairs={{0,8},{4,12},{8,0},{12,4},{1,9},{5,13},{9,1},{13,5},{2,10},{6,14},... | collective-permute-start | bytes 196616 | tf_op jit(solution)/shard_map/ppermute | solution.py:396
  42.0 8.1 %collective-permute-start.16 = (bf16[256,128]{1,0:T(8,128)(2,1)S(1)}, bf16[256,128]{1,0:T(8,128)(2,1)S(1)}, u32[]{:S(2)}, u32[]{:S(2)}) collective-permute-start(bf16[256,128]{1,0:T(8,128)(2,1)S(1)} %get-tuple-element.65), channel_id=1, source_target_pairs={{0,4},{4,8},{8,12},{12,0},{1,5},{5,9},{9,13},{13,1},{2,6},{6,10},{... | collective-permute-start | bytes 196616 | tf_op jit(solution)/shard_map/ppermute | solution.py:396
  43.9 7.0 %collective-permute-start.11 = (bf16[128,128]{1,0:T(8,128)(2,1)S(1)}, bf16[128,128]{1,0:T(8,128)(2,1)S(1)}, u32[]{:S(2)}, u32[]{:S(2)}) collective-permute-start(bf16[128,128]{1,0:T(8,128)(2,1)S(1)} %get-tuple-element.56), channel_id=1, source_target_pairs={{0,12},{4,0},{8,4},{12,8},{1,13},{5,1},{9,5},{13,9},{2,14},{6,2},{... | collective-permute-start | bytes 98312 | tf_op jit(solution)/shard_map/ppermute | solution.py:396
  47.0 4.8 %collective-permute-start.12 = (bf16[128,128]{1,0:T(8,128)(2,1)S(1)}, bf16[128,128]{1,0:T(8,128)(2,1)S(1)}, u32[]{:S(2)}, u32[]{:S(2)}) collective-permute-start(bf16[128,128]{1,0:T(8,128)(2,1)S(1)} %get-tuple-element.57), channel_id=1, source_target_pairs={{0,8},{4,12},{8,0},{12,4},{1,9},{5,13},{9,1},{13,5},{2,10},{6,14},... | collective-permute-start | bytes 98312 | tf_op jit(solution)/shard_map/ppermute | solution.py:396
  50.1 5.7 %collective-permute-start.13 = (bf16[128,128]{1,0:T(8,128)(2,1)S(1)}, bf16[128,128]{1,0:T(8,128)(2,1)S(1)}, u32[]{:S(2)}, u32[]{:S(2)}) collective-permute-start(bf16[128,128]{1,0:T(8,128)(2,1)S(1)} %get-tuple-element.58), channel_id=1, source_target_pairs={{0,4},{4,8},{8,12},{12,0},{1,5},{5,9},{9,13},{13,1},{2,6},{6,10},{... | collective-permute-start | bytes 98312 | tf_op jit(solution)/shard_map/ppermute | solution.py:396

commit v2 on v1

--- a/solution.py
+++ b/solution.py
@@ -153,9 +153,9 @@
     return pl.ds(pl.multiple_of(index * width, width), width)
 
 
-def pack_kernel(n, count_ref, mask_ref, keys_ref, latents_ref, values_ref, weight_ref, cot_ref, *rest):
-    a_outs, v_outs, live_ref = rest[:n], rest[n : 2 * n], rest[2 * n]
-    mask, weight, cot, up_ref, sems = rest[2 * n + 1 :]
+def pack_kernel(n, mask_ref, keys_ref, latents_ref, values_ref, weight_ref, cot_ref, *rest):
+    a_outs, v_outs = rest[:n], rest[n : 2 * n]
+    mask, weight, cot, up_ref, sems = rest[2 * n :]
     me = lax.axis_index("seq")
     tiles, width = v_outs[0].shape
     rows = cot.shape[0]
@@ -165,7 +165,7 @@
         (cot_ref.at[0], cot),
     ]
     for d in range(n):
-        columns = lane_block(lax.rem(me + d, n), width)
+        columns = lane_block((me ^ d), width)
         sources.append((keys_ref.at[0, :, columns], a_outs[d].at[:tiles, :]))
         sources.append((latents_ref.at[:, columns], a_outs[d].at[tiles : tiles + rows, :]))
         sources.append((values_ref.at[0, :, columns], v_outs[d]))
@@ -182,15 +182,11 @@
     for block in range(tiles // BLOCK):
         value = jnp.where(mask[0, block] > 0, 1.0, 0.0)
         flags = jnp.where(row_id == block, value, flags)
-    lane_row = lax.broadcasted_iota(jnp.int32, (1, rows), 1)
-    projected = dot_nt(weight[...], cot[...])
-    up_ref[...] = jnp.where(lane_row + me * rows < count_ref[0], projected, 0.0).astype(bf16)
-    for d in range(n):
-        owner = lax.rem(me + d, n)
+    up_ref[...] = dot_nt(weight[...], cot[...]).astype(bf16)
+    for d in range(n):
+        owner = (me ^ d)
         a_outs[d][tiles + rows : tiles + rows + width, :] = up_ref[lane_block(owner, width), :]
         a_outs[d][tiles + rows + width :, :] = flags.astype(bf16)
-        source_row = lane_row + lax.rem(me + n - d, n) * rows
-        live_ref[:, d * rows : (d + 1) * rows] = jnp.where(source_row < count_ref[0], 1.0, 0.0)
     for copy in copies[3:]:
         copy.wait()
 
@@ -241,7 +237,16 @@
         keys_t_ref[d] = a_refs[d][:tiles, :].astype(f32).T.astype(bf16)
 
 
-def value_grads_kernel(n, heads, expo_ref, total_ref, *refs):
+def live_kernel(n, count_ref, live_ref):
+    me = lax.axis_index("seq")
+    rows = live_ref.shape[1] // n
+    lane_row = lax.broadcasted_iota(jnp.int32, (1, rows), 1)
+    for d in range(n):
+        source_row = lane_row + (me ^ d) * rows
+        live_ref[:, d * rows : (d + 1) * rows] = jnp.where(source_row < count_ref[0], 1.0, 0.0)
+
+
+def value_grads_kernel(n, heads, live_ref, expo_ref, total_ref, *refs):
     a_refs, up_ref, outs = refs[:n], refs[n], refs[n + 1 :]
     factor = HD ** (-0.5)
     width = heads * HD
@@ -249,9 +254,12 @@
     upstream_t = jnp.concatenate(
         [a_refs[d][first : first + width, :] for d in range(n)], axis=1
     )
+    live = live_ref[...] > 0.5
     up_scaled_t = jnp.concatenate(
         [
-            upstream_t[h * HD : (h + 1) * HD, :].astype(f32) * (factor / total_ref[h])
+            jnp.where(
+                live, upstream_t[h * HD : (h + 1) * HD, :].astype(f32) * (factor / total_ref[h]), 0.0
+            )
             for h in range(heads)
         ],
         axis=0,
@@ -322,7 +330,7 @@
     me = lax.axis_index("seq")
     width = c_refs[0].shape[1]
     for d in range(n):
-        value_grad_ref[0, :, lane_block(lax.rem(me + d, n), width)] = c_refs[d][...]
+        value_grad_ref[0, :, lane_block((me ^ d), width)] = c_refs[d][...]
 
 
 def pool_kernel(n, weight_ref, *refs):
@@ -335,7 +343,7 @@
     kept = jnp.zeros(kept_ref.shape, f32)
     sent = jnp.zeros(sent_ref.shape, f32)
     for d in range(n):
-        owner = lax.rem(me + d, n)
+        owner = (me ^ d)
         key_grad_ref[0, :, lane_block(owner, width)] = k_refs[d][:tiles, :]
         attended = k_refs[d][tiles:, :].astype(f32).T.astype(bf16)
         inputs = lane_block(owner, width)
@@ -357,7 +365,7 @@
     me = lax.axis_index("seq")
     width = g_refs[0].shape[0]
     for d in range(n):
-        columns = lane_block(lax.rem(me + d, n), width)
+        columns = lane_block((me ^ d), width)
         latent_grad_ref[:, columns] = g_refs[d][...].astype(f32).T
     pooled_ref[0] = (kept_ref[...] + came_ref[...].astype(f32)).astype(bf16)
 
@@ -391,23 +399,19 @@
     sds = jax.ShapeDtypeStruct
     product = 2 * total_rows * n * tiles * width
 
-    def spread(pieces, sign):
-        return [pieces[0]] + [
-            lax.ppermute(pieces[d], "seq", [(i, (i + sign * d) % n) for i in range(n)])
-            for d in range(1, n)
-        ]
-
-    *packed, live = call(
+    def spread(pieces):
+        came = {0: pieces[0]}
+        for d in offsets(n):
+            came[d] = lax.ppermute(pieces[d], "seq", [(i, i ^ d) for i in range(n)])
+        return [came[d] for d in range(n)]
+
+    packed = call(
         functools.partial(pack_kernel, n),
         [sds((tiles + rows + width + MASK_ROWS, width), bf16)] * n
-        + [sds((tiles, width), bf16)] * n
-        + [sds((1, total_rows), f32)],
-        (
-            latent_counts,
-            *(
-                pltpu.with_memory_space_constraint(x, pltpu.HBM)
-                for x in (tile_mask, tile_keys, latents, tile_values, out_weight, cotangent)
-            ),
+        + [sds((tiles, width), bf16)] * n,
+        tuple(
+            pltpu.with_memory_space_constraint(x, pltpu.HBM)
+            for x in (tile_mask, tile_keys, latents, tile_values, out_weight, cotangent)
         ),
         2 * rows * local_width * out_width,
         [
@@ -417,10 +421,10 @@
             pltpu.VMEM((local_width, rows), bf16),
             pltpu.SemaphoreType.DMA((3 + 3 * n,)),
         ],
-        spaces=[SMEM] + [HBM] * 6,
-    )
-    a_list = spread(packed[:n], 1)
-    v_list = spread(packed[n:], 1)
+        spaces=[HBM] * 6,
+    )
+    a_list = spread(packed[:n])
+    v_list = spread(packed[n:])
     expos, totals, keys_t = call(
         functools.partial(softmax_kernel, n, heads, rows),
         [
@@ -433,15 +437,22 @@
         [pltpu.VMEM((n, tiles, total_rows), f32)],
         16,
     )
+    (live,) = call(
+        functools.partial(live_kernel, n),
+        [sds((1, total_rows), f32)],
+        (latent_counts,),
+        1e4,
+        spaces=[SMEM],
+    )
     up_scaled, *c_out = call(
         functools.partial(value_grads_kernel, n, heads),
         [sds((width, total_rows), bf16)] + [sds((tiles, width), bf16)] * n,
-        (expos, totals, *a_list),
+        (live, expos, totals, *a_list),
         product,
         (),
         16,
     )
-    c_list = spread(c_out, -1)
+    c_list = spread(c_out)
     *k_out, query_grad = call(
         functools.partial(key_grads_kernel, n, heads, rows),
         [sds((tiles + width, width), bf16)] * n + [sds((width, total_rows), bf16)],
@@ -454,14 +465,14 @@
     for step in range(1, sides):
         came = lax.ppermute(query_grad, "slide", [(i, (i + step) % sides) for i in range(sides)])
         other_sum = came if other_sum is None else other_sum.astype(f32) + came.astype(f32)
-    k_list = spread(k_out, -1)
+    k_list = spread(k_out)
     joined = call(
         functools.partial(join_kernel, n),
         [sds((width, rows), bf16)] * n,
         (query_grad, other_sum),
         1e6,
     )
-    g_list = spread(joined, -1)
+    g_list = spread(joined)
     (value_grads,) = call(
         functools.partial(values_home_kernel, n), [sds(tile_values.shape, bf16)], c_list, 1e6
     )
@@ -483,6 +494,10 @@
         1e6,
     )
     return pooled, latent_grads, key_grads, value_grads
+
+
+def offsets(n):
+    return [*range(n // 2, n), *range(n // 2 - 1, 0, -1)]
 
 
 def solution(mesh):
@@ -507,6 +522,8 @@
             and local_width // n == rows
             and tiles % BLOCK == 0
             and tiles // BLOCK <= MASK_ROWS
+            and n >= 4
+            and n & (n - 1) == 0
         )
         if fits:
             return exchanged_body(n, sides, latents, tile_keys, *rest)

time: 56.8 us -> 56.7 us (level)
  waiting for transfers between devices: 24.8 us -> 16.3 us
  starting transfers between devices: 20.8 us -> 29.1 us
    ppermute x15, waiting for transfers between devices: 24.8 us -> 16.3 us  [spread(): came[d] = lax.ppermute(pieces[d], 'seq', [(i, i ^ d) for i in range(n)])]
    ppermute x15, starting transfers between devices: 19.3 us -> 27.6 us  [spread(): came[d] = lax.ppermute(pieces[d], 'seq', [(i, i ^ d) for i in range(n)])]
    pallas_call x8 -> x9, Pallas kernels: 9.66 us -> 9.65 us  [call(): pl.pallas_call(kernel, out_shape=out_shape, in_specs=spaces or [VMEM] * l...]
  transfers between devices with their start and end apart: 17 -> 17, of which waited for: 10 -> 5; matrix products, arithmetic and copies ran while one was open for 0% -> 0% of each run, Pallas kernels for 8% -> 8%
where the time goes in v2:
time: 56.7 us; the launch traced here: 56.5 us
  starting transfers between devices  29.1 us (51%)
  waiting for transfers between devices  16.3 us (29%)
  Pallas kernels  9.65 us (17%)
  between operations  1.36 us (2%)
    ppermute x15, starting transfers between devices, spread(): came[d] = lax.ppermute(pieces[d], 'seq', [(i, i ^ d) for i in range(n)])  27.6 us
    ppermute x15, waiting for transfers between devices, spread(): came[d] = lax.ppermute(pieces[d], 'seq', [(i, i ^ d) for i in range(n)])  16.3 us
    pallas_call x9, Pallas kernels, call(): pl.pallas_call(kernel, out_shape=out_shape, in_specs=spaces or [VMEM] * l...  9.65 us
    ppermute x1, starting transfers between devices, exchanged_body(): lax.ppermute(query_grad, 'slide', [(i, (i + step) % sides) for i in range...  1.49 us
  transfers between devices with their start and end apart: 17, of which 5 were waited for; matrix products, arithmetic and copies ran while one was open for 0% of the time, Pallas kernels for 8%

profile of v2, /device:TPU:0, one launch (start us, length us, event | category | flops | bytes accessed | tf_op | source)
XLA Modules:
  0.0 56.5 jit_solution(10436249093462057301)
XLA Ops:
  0.6 1.9 %shard_map.103 = (bf16[528,128]{1,0:T(8,128)(2,1)S(1)}, bf16[528,128]{1,0:T(8,128)(2,1)S(1)}, bf16[528,128]{1,0:T(8,128)(2,1)S(1)}, bf16[528,128]{1,0:T(8,128)(2...) custom-call(s32[1,2]{1,0:T(1,128)} %mask_ref.1, ...), custom_call_target="tpu_custom_call" | custom-call | flops 134217728 | bytes 2768904 | tf_op jit(solution)/shard_map/pallas_call | solution.py:381
  2.5 3.1 %collective-permute-start = (bf16[528,128]{1,0:T(8,128)(2,1)S(1)}, bf16[528,128]{1,0:T(8,128)(2,1)S(1)}, u32[]{:S(2)}, u32[]{:S(2)}) collective-permute-start(bf16[528,128]{1,0:T(8,128)(2,1)S(1)} %get-tuple-element.35), channel_id=1, source_target_pairs={{0,4},{4,0},{8,12},{12,8},{1,5},{5,1},{9,13},{13,9},{2,6},{6,2},{1... | collective-permute-start | bytes 405512 | tf_op jit(solution)/shard_map/ppermute | solution.py:405
  5.6 2.6 %collective-permute-start.1 = (bf16[528,128]{1,0:T(8,128)(2,1)S(1)}, bf16[528,128]{1,0:T(8,128)(2,1)S(1)}, u32[]{:S(2)}, u32[]{:S(2)}) collective-permute-start(bf16[528,128]{1,0:T(8,128)(2,1)S(1)} %get-tuple-element.36), channel_id=1, source_target_pairs={{0,8},{4,12},{8,0},{12,4},{1,9},{5,13},{9,1},{13,5},{2,10},{6,14},... | collective-permute-start | bytes 405512 | tf_op jit(solution)/shard_map/ppermute | solution.py:405
  8.2 0.0 collective-permute-start.2
  8.2 0.9 %collective-permute-start.3 = (bf16[256,128]{1,0:T(8,128)(2,1)S(1)}, bf16[256,128]{1,0:T(8,128)(2,1)S(1)}, u32[]{:S(2)}, u32[]{:S(2)}) collective-permute-start(bf16[256,128]{1,0:T(8,128)(2,1)S(1)} %get-tuple-element.43), channel_id=1, source_target_pairs={{0,4},{4,0},{8,12},{12,8},{1,5},{5,1},{9,13},{13,9},{2,6},{6,2},{1... | collective-permute-start | bytes 196616 | tf_op jit(solution)/shard_map/ppermute | solution.py:405
  9.1 3.5 %collective-permute-start.4 = (bf16[256,128]{1,0:T(8,128)(2,1)S(1)}, bf16[256,128]{1,0:T(8,128)(2,1)S(1)}, u32[]{:S(2)}, u32[]{:S(2)}) collective-permute-start(bf16[256,128]{1,0:T(8,128)(2,1)S(1)} %get-tuple-element.44), channel_id=1, source_target_pairs={{0,8},{4,12},{8,0},{12,4},{1,9},{5,13},{9,1},{13,5},{2,10},{6,14},... | collective-permute-start | bytes 196616 | tf_op jit(solution)/shard_map/ppermute | solution.py:405
  12.6 0.0 collective-permute-done.refs_1_
  12.6 3.2 %collective-permute-start.5 = (bf16[256,128]{1,0:T(8,128)(2,1)S(1)}, bf16[256,128]{1,0:T(8,128)(2,1)S(1)}, u32[]{:S(2)}, u32[]{:S(2)}) collective-permute-start(bf16[256,128]{1,0:T(8,128)(2,1)S(1)} %get-tuple-element.45), channel_id=1, source_target_pairs={{0,12},{4,8},{8,4},{12,0},{1,13},{5,9},{9,5},{13,1},{2,14},{6,10},... | collective-permute-start | bytes 196616 | tf_op jit(solution)/shard_map/ppermute | solution.py:405
  16.5 5.1 %collective-permute-done.1.refs_2_ = bf16[528,128]{1,0:T(8,128)(2,1)S(1)} collective-permute-done((bf16[528,128]{1,0:T(8,128)(2,1)S(1)}, bf16[528,128]{1,0:T(8,128)(2,1)S(1)}, u32[]{:S(2)}, u32[]{:S(2)}) %collective-permute-start.1) | collective-permute-done | bytes 135200 | tf_op jit(solution)/shard_map/ppermute | solution.py:405
  21.6 0.0 collective-permute-done.2.refs_3_
  21.6 1.6 %shard_map.104 = (bf16[2,4,256,512]{3,2,1,0:T(8,128)(2,1)S(1)}, f32[2,1,512]{2,1,0:T(1,128)S(1)}, bf16[4,128,256]{2,1,0:T(8,128)(2,1)S(1)}) custom-call(bf16[528,128]{1,0:T(8,128)(2,1)S(1)} %get-tuple-element.34.refs_0_, bf16[528,128]{1,0:T(8,128)(2,1)S(1)} %collective-permute-done.refs_1_, bf16[528,128]{1,0:T(8,128)(2,1)S(1)} %collective-permute-done.1.refs_2_, ...), custom_call_target="tpu_custom_call" | custom-call | flops 134217728 | bytes 2904064 | tf_op jit(solution)/shard_map/pallas_call | solution.py:381
  23.2 0.8 %shard_map.105 = (bf16[128,512]{1,0:T(8,128)(2,1)S(1)}, bf16[256,128]{1,0:T(8,128)(2,1)S(1)}, bf16[256,128]{1,0:T(8,128)(2,1)S(1)}, bf16[256,128]{1,0:T(8,128)(2,1)S(1)}, bf16[256,128]{1,0:T(8,128)(2,1)S(1)}) custom-call(f32[1,512]{1,0:T(1,128)S(1)} %shard_map.102.live_ref, bf16[2,4,256,512]{3,2,1,0:T(8,128)(2,1)S(1)} %get-tuple-element.38.expo_ref, ...), custom_call_target="tpu_custom_call" | custom-call | flops 134217728 | bytes 3037184 | tf_op jit(solution)/shard_map/pallas_call | solution.py:381
  24.0 0.0 copy-start
  24.0 0.0 collective-permute-done.3.refs_5_
  24.0 1.2 %collective-permute-done.4.refs_6_ = bf16[256,128]{1,0:T(8,128)(2,1)S(1)} collective-permute-done((bf16[256,128]{1,0:T(8,128)(2,1)S(1)}, bf16[256,128]{1,0:T(8,128)(2,1)S(1)}, u32[]{:S(2)}, u32[]{:S(2)}) %collective-permute-start.4) | collective-permute-done | bytes 65568 | tf_op jit(solution)/shard_map/ppermute | solution.py:405
  25.2 0.0 collective-permute-done.5.refs_7_
  25.2 2.6 %shard_map.106 = (bf16[384,128]{1,0:T(8,128)(2,1)S(1)}, bf16[384,128]{1,0:T(8,128)(2,1)S(1)}, bf16[384,128]{1,0:T(8,128)(2,1)S(1)}, bf16[384,128]{1,0:T(8,128)(2,1)S(1)}, bf16[128,512]{1,0:T(8,128)(2,1)S(1)}) custom-call(f32[1,512]{1,0:T(1,128)S(1)} %shard_map.102.live_ref, bf16[2,4,256,512]{3,2,1,0:T(8,128)(2,1)S(1)} %get-tuple-element.38.expo_ref, ...), custom_call_target="tpu_custom_call" | custom-call | flops 536870912 | bytes 3823616 | tf_op jit(solution)/shard_map/pallas_call | solution.py:381
  27.8 2.4 %collective-permute-start.6 = (bf16[384,128]{1,0:T(8,128)(2,1)S(1)}, bf16[384,128]{1,0:T(8,128)(2,1)S(1)}, u32[]{:S(2)}, u32[]{:S(2)}) collective-permute-start(bf16[384,128]{1,0:T(8,128)(2,1)S(1)} %get-tuple-element.47), channel_id=1, source_target_pairs={{0,4},{4,0},{8,12},{12,8},{1,5},{5,1},{9,13},{13,9},{2,6},{6,2},{1... | collective-permute-start | bytes 294920 | tf_op jit(solution)/shard_map/ppermute | solution.py:405
  30.2 0.9 %collective-permute-start.7 = (bf16[384,128]{1,0:T(8,128)(2,1)S(1)}, bf16[384,128]{1,0:T(8,128)(2,1)S(1)}, u32[]{:S(2)}, u32[]{:S(2)}) collective-permute-start(bf16[384,128]{1,0:T(8,128)(2,1)S(1)} %get-tuple-element.48), channel_id=1, source_target_pairs={{0,8},{4,12},{8,0},{12,4},{1,9},{5,13},{9,1},{13,5},{2,10},{6,14},... | collective-permute-start | bytes 294920 | tf_op jit(solution)/shard_map/ppermute | solution.py:405
  31.1 1.5 %collective-permute-start.8 = (bf16[384,128]{1,0:T(8,128)(2,1)S(1)}, bf16[384,128]{1,0:T(8,128)(2,1)S(1)}, u32[]{:S(2)}, u32[]{:S(2)}) collective-permute-start(bf16[384,128]{1,0:T(8,128)(2,1)S(1)} %get-tuple-element.49), channel_id=1, source_target_pairs={{0,12},{4,8},{8,4},{12,0},{1,13},{5,9},{9,5},{13,1},{2,14},{6,10},... | collective-permute-start | bytes 294920 | tf_op jit(solution)/shard_map/ppermute | solution.py:405
  32.6 1.5 %collective-permute-start.10 = (bf16[128,512]{1,0:T(8,128)(2,1)S(1)}, bf16[128,512]{1,0:T(8,128)(2,1)S(1)}, u32[]{:S(2)}, u32[]{:S(2)}) collective-permute-start(bf16[128,512]{1,0:T(8,128)(2,1)S(1)} %get-tuple-element.52.own_ref), channel_id=1, source_target_pairs={{0,2},{2,0},{1,3},{3,1},{4,6},{6,4},{5,7},{7,5},{8,10},{10,8},{9,1... | collective-permute-start | bytes 393224 | tf_op jit(solution)/shard_map/ppermute | solution.py:466
  34.1 0.0 collective-permute-done.6.refs_1_
  34.1 4.3 %collective-permute-done.7.refs_2_ = bf16[384,128]{1,0:T(8,128)(2,1)S(1)} collective-permute-done((bf16[384,128]{1,0:T(8,128)(2,1)S(1)}, bf16[384,128]{1,0:T(8,128)(2,1)S(1)}, u32[]{:S(2)}, u32[]{:S(2)}) %collective-permute-start.7) | collective-permute-done | bytes 98336 | tf_op jit(solution)/shard_map/ppermute | solution.py:405
  38.4 0.0 collective-permute-done.8.refs_3_
  38.4 0.0 copy-done
  38.4 1.1 %shard_map.107 = (bf16[1,256,512]{2,1,0:T(8,128)(2,1)}, f32[128,512]{1,0:T(8,128)S(1)}, bf16[128,512]{1,0:T(8,128)(2,1)S(1)}) custom-call(bf16[512,1024]{1,0:T(8,128)(2,1)S(1)} %copy-done, bf16[384,128]{1,0:T(8,128)(2,1)S(1)} %get-tuple-element.46.refs_0_, bf16[384,128]{1,0:T(8,128)(2,1)S(1)} %collective-permute-done.6.refs_1_, ...), custom_call_target="tpu_custom_call" | custom-call | flops 134217728 | bytes 2097152 | tf_op jit(solution)/shard_map/pallas_call | solution.py:381
  39.5 0.0 collective-permute-start.9
  39.5 1.6 %collective-permute-start.14 = (bf16[256,128]{1,0:T(8,128)(2,1)S(1)}, bf16[256,128]{1,0:T(8,128)(2,1)S(1)}, u32[]{:S(2)}, u32[]{:S(2)}) collective-permute-start(bf16[256,128]{1,0:T(8,128)(2,1)S(1)} %get-tuple-element.61), channel_id=1, source_target_pairs={{0,4},{4,0},{8,12},{12,8},{1,5},{5,1},{9,13},{13,9},{2,6},{6,2},{1... | collective-permute-start | bytes 196616 | tf_op jit(solution)/shard_map/ppermute | solution.py:405
  41.1 1.3 %collective-permute-start.15 = (bf16[256,128]{1,0:T(8,128)(2,1)S(1)}, bf16[256,128]{1,0:T(8,128)(2,1)S(1)}, u32[]{:S(2)}, u32[]{:S(2)}) collective-permute-start(bf16[256,128]{1,0:T(8,128)(2,1)S(1)} %get-tuple-element.62), channel_id=1, source_target_pairs={{0,8},{4,12},{8,0},{12,4},{1,9},{5,13},{9,1},{13,5},{2,10},{6,14},... | collective-permute-start | bytes 196616 | tf_op jit(solution)/shard_map/ppermute | solution.py:405
  42.4 1.5 %collective-permute-start.16 = (bf16[256,128]{1,0:T(8,128)(2,1)S(1)}, bf16[256,128]{1,0:T(8,128)(2,1)S(1)}, u32[]{:S(2)}, u32[]{:S(2)}) collective-permute-start(bf16[256,128]{1,0:T(8,128)(2,1)S(1)} %get-tuple-element.63), channel_id=1, source_target_pairs={{0,12},{4,8},{8,4},{12,0},{1,13},{5,9},{9,5},{13,1},{2,14},{6,10},... | collective-permute-start | bytes 196616 | tf_op jit(solution)/shard_map/ppermute | solution.py:405
  43.9 0.0 collective-permute-done.10.other_ref
  44.0 0.8 %collective-permute-start.11 = (bf16[128,128]{1,0:T(8,128)(2,1)S(1)}, bf16[128,128]{1,0:T(8,128)(2,1)S(1)}, u32[]{:S(2)}, u32[]{:S(2)}) collective-permute-start(bf16[128,128]{1,0:T(8,128)(2,1)S(1)} %get-tuple-element.54), channel_id=1, source_target_pairs={{0,4},{4,0},{8,12},{12,8},{1,5},{5,1},{9,13},{13,9},{2,6},{6,2},{1... | collective-permute-start | bytes 98312 | tf_op jit(solution)/shard_map/ppermute | solution.py:405
  44.7 0.0 collective-permute-done.14.refs_1_
  44.8 2.2 %collective-permute-start.12 = (bf16[128,128]{1,0:T(8,128)(2,1)S(1)}, bf16[128,128]{1,0:T(8,128)(2,1)S(1)}, u32[]{:S(2)}, u32[]{:S(2)}) collective-permute-start(bf16[128,128]{1,0:T(8,128)(2,1)S(1)} %get-tuple-element.55), channel_id=1, source_target_pairs={{0,8},{4,12},{8,0},{12,4},{1,9},{5,13},{9,1},{13,5},{2,10},{6,14},... | collective-permute-start | bytes 98312 | tf_op jit(solution)/shard_map/ppermute | solution.py:405
  47.0 3.0 %collective-permute-done.15.refs_2_ = bf16[256,128]{1,0:T(8,128)(2,1)S(1)} collective-permute-done((bf16[256,128]{1,0:T(8,128)(2,1)S(1)}, bf16[256,128]{1,0:T(8,128)(2,1)S(1)}, u32[]{:S(2)}, u32[]{:S(2)}) %collective-permute-start.15) | collective-permute-done | bytes 65568 | tf_op jit(solution)/shard_map/ppermute | solution.py:405
  49.9 2.2 %collective-permute-start.13 = (bf16[128,128]{1,0:T(8,128)(2,1)S(1)}, bf16[128,128]{1,0:T(8,128)(2,1)S(1)}, u32[]{:S(2)}, u32[]{:S(2)}) collective-permute-start(bf16[128,128]{1,0:T(8,128)(2,1)S(1)} %get-tuple-element.56), channel_id=1, source_target_pairs={{0,12},{4,8},{8,4},{12,0},{1,13},{5,9},{9,5},{13,1},{2,14},{6,10},... | collective-permute-start | bytes 98312 | tf_op jit(solution)/shard_map/ppermute | solution.py:405
  52.1 0.0 collective-permute-done.16.refs_3_
  52.1 0.8 %shard_map.110 = bf16[1,256,512]{2,1,0:T(8,128)(2,1)} custom-call(bf16[256,128]{1,0:T(8,128)(2,1)S(1)} %get-tuple-element.60.refs_0_, bf16[256,128]{1,0:T(8,128)(2,1)S(1)} %collective-permute-done.14.refs_1_, bf16[256,128]{1,0:T(8,128)(2,1)S(1)} %collective-permute-done.15.refs_2_, bf16[256,128]{1,0:T(8,128)(2,1)S(1)} %collective-permute-done.16.refs_3_), custom_call_target="tpu_custom_call" | custom-call | flops 1000000 | bytes 524288 | tf_op jit(solution)/shard_map/pallas_call | solution.py:381
  52.9 0.0 collective-permute-done.11.refs_1_
  52.9 0.0 collective-permute-done.12.refs_2_
  52.9 2.8 %collective-permute-done.13.refs_3_ = bf16[128,128]{1,0:T(8,128)(2,1)S(1)} collective-permute-done((bf16[128,128]{1,0:T(8,128)(2,1)S(1)}, bf16[128,128]{1,0:T(8,128)(2,1)S(1)}, u32[]{:S(2)}, u32[]{:S(2)}) %collective-permute-start.13) | collective-permute-done | bytes 32800 | tf_op jit(solution)/shard_map/ppermute | solution.py:405
  55.7 0.0 collective-permute-done.9.came_ref
  55.7 0.8 %shard_map.109 = (f32[128,512]{1,0:T(8,128)}, bf16[1,128,512]{2,1,0:T(8,128)(2,1)}) custom-call(f32[128,512]{1,0:T(8,128)S(1)} %get-tuple-element.50.kept_ref, bf16[128,512]{1,0:T(8,128)(2,1)S(1)} %collective-permute-done.9.came_ref, bf16[128,128]{1,0:T(8,128)(2,1)S(1)} %get-tuple-element.53.refs_0_, bf16[128,128]{1,0:T(8,128)(2,1)S(1)} %collective-permute-done.11.refs_1_, ...), custom_call_target="tpu_custom_call" | custom-call | flops 1000000 | bytes 917504 | tf_op jit(solution)/shard_map/pallas_call | solution.py:381
  (2 shorter events, 0.1 us)
Async XLA Ops:
  2.5 10.1 %collective-permute-start = (bf16[528,128]{1,0:T(8,128)(2,1)S(1)}, bf16[528,128]{1,0:T(8,128)(2,1)S(1)}, u32[]{:S(2)}, u32[]{:S(2)}) collective-permute-start(bf16[528,128]{1,0:T(8,128)(2,1)S(1)} %get-tuple-element.35), channel_id=1, source_target_pairs={{0,4},{4,0},{8,12},{12,8},{1,5},{5,1},{9,13},{13,9},{2,6},{6,2},{1... | collective-permute-start | bytes 405512 | tf_op jit(solution)/shard_map/ppermute | solution.py:405
  5.6 16.0 %collective-permute-start.1 = (bf16[528,128]{1,0:T(8,128)(2,1)S(1)}, bf16[528,128]{1,0:T(8,128)(2,1)S(1)}, u32[]{:S(2)}, u32[]{:S(2)}) collective-permute-start(bf16[528,128]{1,0:T(8,128)(2,1)S(1)} %get-tuple-element.36), channel_id=1, source_target_pairs={{0,8},{4,12},{8,0},{12,4},{1,9},{5,13},{9,1},{13,5},{2,10},{6,14},... | collective-permute-start | bytes 405512 | tf_op jit(solution)/shard_map/ppermute | solution.py:405
  8.2 13.4 %collective-permute-start.2 = (bf16[528,128]{1,0:T(8,128)(2,1)S(1)}, bf16[528,128]{1,0:T(8,128)(2,1)S(1)}, u32[]{:S(2)}, u32[]{:S(2)}) collective-permute-start(bf16[528,128]{1,0:T(8,128)(2,1)S(1)} %get-tuple-element.37), channel_id=1, source_target_pairs={{0,12},{4,8},{8,4},{12,0},{1,13},{5,9},{9,5},{13,1},{2,14},{6,10},... | collective-permute-start | bytes 405512 | tf_op jit(solution)/shard_map/ppermute | solution.py:405
  8.2 15.8 %collective-permute-start.3 = (bf16[256,128]{1,0:T(8,128)(2,1)S(1)}, bf16[256,128]{1,0:T(8,128)(2,1)S(1)}, u32[]{:S(2)}, u32[]{:S(2)}) collective-permute-start(bf16[256,128]{1,0:T(8,128)(2,1)S(1)} %get-tuple-element.43), channel_id=1, source_target_pairs={{0,4},{4,0},{8,12},{12,8},{1,5},{5,1},{9,13},{13,9},{2,6},{6,2},{1... | collective-permute-start | bytes 196616 | tf_op jit(solution)/shard_map/ppermute | solution.py:405
  9.1 16.1 %collective-permute-start.4 = (bf16[256,128]{1,0:T(8,128)(2,1)S(1)}, bf16[256,128]{1,0:T(8,128)(2,1)S(1)}, u32[]{:S(2)}, u32[]{:S(2)}) collective-permute-start(bf16[256,128]{1,0:T(8,128)(2,1)S(1)} %get-tuple-element.44), channel_id=1, source_target_pairs={{0,8},{4,12},{8,0},{12,4},{1,9},{5,13},{9,1},{13,5},{2,10},{6,14},... | collective-permute-start | bytes 196616 | tf_op jit(solution)/shard_map/ppermute | solution.py:405
  12.6 12.6 %collective-permute-start.5 = (bf16[256,128]{1,0:T(8,128)(2,1)S(1)}, bf16[256,128]{1,0:T(8,128)(2,1)S(1)}, u32[]{:S(2)}, u32[]{:S(2)}) collective-permute-start(bf16[256,128]{1,0:T(8,128)(2,1)S(1)} %get-tuple-element.45), channel_id=1, source_target_pairs={{0,12},{4,8},{8,4},{12,0},{1,13},{5,9},{9,5},{13,1},{2,14},{6,10},... | collective-permute-start | bytes 196616 | tf_op jit(solution)/shard_map/ppermute | solution.py:405
  24.0 14.4 %copy-start = (bf16[512,1024]{1,0:T(8,128)(2,1)S(1)}, bf16[512,1024]{1,0:T(8,128)(2,1)}, u32[]{:S(2)}) copy-start(bf16[512,1024]{1,0:T(8,128)(2,1)} %weight_ref.3) | copy-start | bytes 3145732
  27.8 6.3 %collective-permute-start.6 = (bf16[384,128]{1,0:T(8,128)(2,1)S(1)}, bf16[384,128]{1,0:T(8,128)(2,1)S(1)}, u32[]{:S(2)}, u32[]{:S(2)}) collective-permute-start(bf16[384,128]{1,0:T(8,128)(2,1)S(1)} %get-tuple-element.47), channel_id=1, source_target_pairs={{0,4},{4,0},{8,12},{12,8},{1,5},{5,1},{9,13},{13,9},{2,6},{6,2},{1... | collective-permute-start | bytes 294920 | tf_op jit(solution)/shard_map/ppermute | solution.py:405
  30.2 8.2 %collective-permute-start.7 = (bf16[384,128]{1,0:T(8,128)(2,1)S(1)}, bf16[384,128]{1,0:T(8,128)(2,1)S(1)}, u32[]{:S(2)}, u32[]{:S(2)}) collective-permute-start(bf16[384,128]{1,0:T(8,128)(2,1)S(1)} %get-tuple-element.48), channel_id=1, source_target_pairs={{0,8},{4,12},{8,0},{12,4},{1,9},{5,13},{9,1},{13,5},{2,10},{6,14},... | collective-permute-start | bytes 294920 | tf_op jit(solution)/shard_map/ppermute | solution.py:405
  31.1 7.3 %collective-permute-start.8 = (bf16[384,128]{1,0:T(8,128)(2,1)S(1)}, bf16[384,128]{1,0:T(8,128)(2,1)S(1)}, u32[]{:S(2)}, u32[]{:S(2)}) collective-permute-start(bf16[384,128]{1,0:T(8,128)(2,1)S(1)} %get-tuple-element.49), channel_id=1, source_target_pairs={{0,12},{4,8},{8,4},{12,0},{1,13},{5,9},{9,5},{13,1},{2,14},{6,10},... | collective-permute-start | bytes 294920 | tf_op jit(solution)/shard_map/ppermute | solution.py:405
  32.6 11.3 %collective-permute-start.10 = (bf16[128,512]{1,0:T(8,128)(2,1)S(1)}, bf16[128,512]{1,0:T(8,128)(2,1)S(1)}, u32[]{:S(2)}, u32[]{:S(2)}) collective-permute-start(bf16[128,512]{1,0:T(8,128)(2,1)S(1)} %get-tuple-element.52.own_ref), channel_id=1, source_target_pairs={{0,2},{2,0},{1,3},{3,1},{4,6},{6,4},{5,7},{7,5},{8,10},{10,8},{9,1... | collective-permute-start | bytes 393224 | tf_op jit(solution)/shard_map/ppermute | solution.py:466
  39.5 16.1 %collective-permute-start.9 = (bf16[128,512]{1,0:T(8,128)(2,1)S(1)}, bf16[128,512]{1,0:T(8,128)(2,1)S(1)}, u32[]{:S(2)}, u32[]{:S(2)}) collective-permute-start(bf16[128,512]{1,0:T(8,128)(2,1)S(1)} %get-tuple-element.51), channel_id=1, source_target_pairs={{0,1},{1,0},{2,3},{3,2},{4,5},{5,4},{6,7},{7,6},{8,9},{9,8},{10,11... | collective-permute-start | bytes 393224 | tf_op jit(solution)/shard_map/ppermute | solution.py:489
  39.5 5.2 %collective-permute-start.14 = (bf16[256,128]{1,0:T(8,128)(2,1)S(1)}, bf16[256,128]{1,0:T(8,128)(2,1)S(1)}, u32[]{:S(2)}, u32[]{:S(2)}) collective-permute-start(bf16[256,128]{1,0:T(8,128)(2,1)S(1)} %get-tuple-element.61), channel_id=1, source_target_pairs={{0,4},{4,0},{8,12},{12,8},{1,5},{5,1},{9,13},{13,9},{2,6},{6,2},{1... | collective-permute-start | bytes 196616 | tf_op jit(solution)/shard_map/ppermute | solution.py:405
  41.1 8.8 %collective-permute-start.15 = (bf16[256,128]{1,0:T(8,128)(2,1)S(1)}, bf16[256,128]{1,0:T(8,128)(2,1)S(1)}, u32[]{:S(2)}, u32[]{:S(2)}) collective-permute-start(bf16[256,128]{1,0:T(8,128)(2,1)S(1)} %get-tuple-element.62), channel_id=1, source_target_pairs={{0,8},{4,12},{8,0},{12,4},{1,9},{5,13},{9,1},{13,5},{2,10},{6,14},... | collective-permute-start | bytes 196616 | tf_op jit(solution)/shard_map/ppermute | solution.py:405
  42.4 9.7 %collective-permute-start.16 = (bf16[256,128]{1,0:T(8,128)(2,1)S(1)}, bf16[256,128]{1,0:T(8,128)(2,1)S(1)}, u32[]{:S(2)}, u32[]{:S(2)}) collective-permute-start(bf16[256,128]{1,0:T(8,128)(2,1)S(1)} %get-tuple-element.63), channel_id=1, source_target_pairs={{0,12},{4,8},{8,4},{12,0},{1,13},{5,9},{9,5},{13,1},{2,14},{6,10},... | collective-permute-start | bytes 196616 | tf_op jit(solution)/shard_map/ppermute | solution.py:405
  44.0 8.9 %collective-permute-start.11 = (bf16[128,128]{1,0:T(8,128)(2,1)S(1)}, bf16[128,128]{1,0:T(8,128)(2,1)S(1)}, u32[]{:S(2)}, u32[]{:S(2)}) collective-permute-start(bf16[128,128]{1,0:T(8,128)(2,1)S(1)} %get-tuple-element.54), channel_id=1, source_target_pairs={{0,4},{4,0},{8,12},{12,8},{1,5},{5,1},{9,13},{13,9},{2,6},{6,2},{1... | collective-permute-start | bytes 98312 | tf_op jit(solution)/shard_map/ppermute | solution.py:405
  44.8 8.1 %collective-permute-start.12 = (bf16[128,128]{1,0:T(8,128)(2,1)S(1)}, bf16[128,128]{1,0:T(8,128)(2,1)S(1)}, u32[]{:S(2)}, u32[]{:S(2)}) collective-permute-start(bf16[128,128]{1,0:T(8,128)(2,1)S(1)} %get-tuple-element.55), channel_id=1, source_target_pairs={{0,8},{4,12},{8,0},{12,4},{1,9},{5,13},{9,1},{13,5},{2,10},{6,14},... | collective-permute-start | bytes 98312 | tf_op jit(solution)/shard_map/ppermute | solution.py:405
  49.9 5.7 %collective-permute-start.13 = (bf16[128,128]{1,0:T(8,128)(2,1)S(1)}, bf16[128,128]{1,0:T(8,128)(2,1)S(1)}, u32[]{:S(2)}, u32[]{:S(2)}) collective-permute-start(bf16[128,128]{1,0:T(8,128)(2,1)S(1)} %get-tuple-element.56), channel_id=1, source_target_pairs={{0,12},{4,8},{8,4},{12,0},{1,13},{5,9},{9,5},{13,1},{2,14},{6,10},... | collective-permute-start | bytes 98312 | tf_op jit(solution)/shard_map/ppermute | solution.py:405

commit v3 on v2

--- a/solution.py
+++ b/solution.py
@@ -153,41 +153,57 @@
     return pl.ds(pl.multiple_of(index * width, width), width)
 
 
-def pack_kernel(n, mask_ref, keys_ref, latents_ref, values_ref, weight_ref, cot_ref, *rest):
-    a_outs, v_outs = rest[:n], rest[n : 2 * n]
-    mask, weight, cot, up_ref, sems = rest[2 * n :]
+def pack_keys_kernel(n, mask_ref, keys_ref, latents_ref, *rest):
+    outs, mask, sems = rest[:n], rest[n], rest[n + 1]
     me = lax.axis_index("seq")
-    tiles, width = v_outs[0].shape
-    rows = cot.shape[0]
-    sources = [
-        (mask_ref, mask),
-        (weight_ref, weight),
-        (cot_ref.at[0], cot),
-    ]
-    for d in range(n):
-        columns = lane_block((me ^ d), width)
-        sources.append((keys_ref.at[0, :, columns], a_outs[d].at[:tiles, :]))
-        sources.append((latents_ref.at[:, columns], a_outs[d].at[tiles : tiles + rows, :]))
-        sources.append((values_ref.at[0, :, columns], v_outs[d]))
+    tiles, rows, width = keys_ref.shape[1], latents_ref.shape[0], outs[0].shape[1]
+    sources = [(mask_ref, mask)]
+    for d in range(n):
+        columns = lane_block(me ^ d, width)
+        sources.append((keys_ref.at[0, :, columns], outs[d].at[:tiles, :]))
+        sources.append((latents_ref.at[:, columns], outs[d].at[tiles : tiles + rows, :]))
     copies = [
         pltpu.make_async_copy(source, target, sems.at[i])
         for i, (source, target) in enumerate(sources)
     ]
     for copy in copies:
         copy.start()
-    for copy in copies[:3]:
-        copy.wait()
+    copies[0].wait()
     row_id = lax.broadcasted_iota(jnp.int32, (MASK_ROWS, width), 0)
     flags = jnp.zeros((MASK_ROWS, width), f32)
     for block in range(tiles // BLOCK):
         value = jnp.where(mask[0, block] > 0, 1.0, 0.0)
         flags = jnp.where(row_id == block, value, flags)
+    for d in range(n):
+        outs[d][tiles + rows :, :] = flags.astype(bf16)
+    for copy in copies[1:]:
+        copy.wait()
+
+
+def pack_values_kernel(n, count_ref, values_ref, weight_ref, cot_ref, *rest):
+    u_outs, v_outs, live_ref = rest[:n], rest[n : 2 * n], rest[2 * n]
+    weight, cot, up_ref, sems = rest[2 * n + 1 :]
+    me = lax.axis_index("seq")
+    width, rows = u_outs[0].shape
+    sources = [(weight_ref, weight), (cot_ref.at[0], cot)]
+    for d in range(n):
+        sources.append((values_ref.at[0, :, lane_block(me ^ d, width)], v_outs[d]))
+    copies = [
+        pltpu.make_async_copy(source, target, sems.at[i])
+        for i, (source, target) in enumerate(sources)
+    ]
+    for copy in copies:
+        copy.start()
+    lane_row = lax.broadcasted_iota(jnp.int32, (1, rows), 1)
+    for d in range(n):
+        source_row = lane_row + (me ^ d) * rows
+        live_ref[:, d * rows : (d + 1) * rows] = jnp.where(source_row < count_ref[0], 1.0, 0.0)
+    for copy in copies[:2]:
+        copy.wait()
     up_ref[...] = dot_nt(weight[...], cot[...]).astype(bf16)
     for d in range(n):
-        owner = (me ^ d)
-        a_outs[d][tiles + rows : tiles + rows + width, :] = up_ref[lane_block(owner, width), :]
-        a_outs[d][tiles + rows + width :, :] = flags.astype(bf16)
-    for copy in copies[3:]:
+        u_outs[d][...] = up_ref[lane_block(me ^ d, width), :]
+    for copy in copies[2:]:
         copy.wait()
 
 
@@ -207,7 +223,7 @@
     queries_t = queries.astype(f32).T.astype(bf16)
     valid = []
     for d in range(n):
-        flags = a_refs[d][tiles + rows + width :, :].astype(f32)
+        flags = a_refs[d][tiles + rows :, :].astype(f32)
         for j in range(per_block):
             valid.append(
                 jnp.concatenate([flags[j : j + 1, :]] * (total_rows // width), axis=1) > 0.5
@@ -237,23 +253,10 @@
         keys_t_ref[d] = a_refs[d][:tiles, :].astype(f32).T.astype(bf16)
 
 
-def live_kernel(n, count_ref, live_ref):
-    me = lax.axis_index("seq")
-    rows = live_ref.shape[1] // n
-    lane_row = lax.broadcasted_iota(jnp.int32, (1, rows), 1)
-    for d in range(n):
-        source_row = lane_row + (me ^ d) * rows
-        live_ref[:, d * rows : (d + 1) * rows] = jnp.where(source_row < count_ref[0], 1.0, 0.0)
-
-
 def value_grads_kernel(n, heads, live_ref, expo_ref, total_ref, *refs):
-    a_refs, up_ref, outs = refs[:n], refs[n], refs[n + 1 :]
+    u_refs, up_ref, outs = refs[:n], refs[n], refs[n + 1 :]
     factor = HD ** (-0.5)
-    width = heads * HD
-    first = a_refs[0].shape[0] - MASK_ROWS - width
-    upstream_t = jnp.concatenate(
-        [a_refs[d][first : first + width, :] for d in range(n)], axis=1
-    )
+    upstream_t = jnp.concatenate([u_refs[d][...] for d in range(n)], axis=1)
     live = live_ref[...] > 0.5
     up_scaled_t = jnp.concatenate(
         [
@@ -405,25 +408,34 @@
             came[d] = lax.ppermute(pieces[d], "seq", [(i, i ^ d) for i in range(n)])
         return [came[d] for d in range(n)]
 
+    def in_hbm(*arrays):
+        return tuple(pltpu.with_memory_space_constraint(x, pltpu.HBM) for x in arrays)
+
     packed = call(
-        functools.partial(pack_kernel, n),
-        [sds((tiles + rows + width + MASK_ROWS, width), bf16)] * n
-        + [sds((tiles, width), bf16)] * n,
-        tuple(
-            pltpu.with_memory_space_constraint(x, pltpu.HBM)
-            for x in (tile_mask, tile_keys, latents, tile_values, out_weight, cotangent)
-        ),
+        functools.partial(pack_keys_kernel, n),
+        [sds((tiles + rows + MASK_ROWS, width), bf16)] * n,
+        in_hbm(tile_mask, tile_keys, latents),
+        1e6,
+        [pltpu.SMEM(tile_mask.shape, jnp.int32), pltpu.SemaphoreType.DMA((1 + 2 * n,))],
+        spaces=[HBM] * 3,
+    )
+    a_list = spread(packed)
+    *packed, live = call(
+        functools.partial(pack_values_kernel, n),
+        [sds((width, rows), bf16)] * n
+        + [sds((tiles, width), bf16)] * n
+        + [sds((1, total_rows), f32)],
+        (latent_counts, *in_hbm(tile_values, out_weight, cotangent)),
         2 * rows * local_width * out_width,
         [
-            pltpu.SMEM(tile_mask.shape, jnp.int32),
             pltpu.VMEM(out_weight.shape, bf16),
             pltpu.VMEM(cotangent.shape[1:], bf16),
             pltpu.VMEM((local_width, rows), bf16),
-            pltpu.SemaphoreType.DMA((3 + 3 * n,)),
+            pltpu.SemaphoreType.DMA((2 + n,)),
         ],
-        spaces=[HBM] * 6,
-    )
-    a_list = spread(packed[:n])
+        spaces=[SMEM] + [HBM] * 3,
+    )
+    u_list = spread(packed[:n])
     v_list = spread(packed[n:])
     expos, totals, keys_t = call(
         functools.partial(softmax_kernel, n, heads, rows),
@@ -437,17 +449,10 @@
         [pltpu.VMEM((n, tiles, total_rows), f32)],
         16,
     )
-    (live,) = call(
-        functools.partial(live_kernel, n),
-        [sds((1, total_rows), f32)],
-        (latent_counts,),
-        1e4,
-        spaces=[SMEM],
-    )
     up_scaled, *c_out = call(
         functools.partial(value_grads_kernel, n, heads),
         [sds((width, total_rows), bf16)] + [sds((tiles, width), bf16)] * n,
-        (live, expos, totals, *a_list),
+        (live, expos, totals, *u_list),
         product,
         (),
         16,

time: 56.7 us -> 57.5 us (1.014)
  Pallas kernels: 9.65 us -> 10.6 us
    pallas_call x9, Pallas kernels: 9.65 us -> 10.6 us  [call(): pl.pallas_call(kernel, out_shape=out_shape, in_specs=spaces or [VMEM] * l...]
    ppermute x15 -> x18, starting transfers between devices: 27.6 us -> 27.4 us  [spread(): came[d] = lax.ppermute(pieces[d], 'seq', [(i, i ^ d) for i in range(n)])]
    ppermute x15 -> x18, waiting for transfers between devices: 16.3 us -> 16.3 us  [spread(): came[d] = lax.ppermute(pieces[d], 'seq', [(i, i ^ d) for i in range(n)])]
  transfers between devices with their start and end apart: 17 -> 20, of which waited for: 5 -> 7; matrix products, arithmetic and copies ran while one was open for 0% -> 0% of each run, Pallas kernels for 8% -> 11%
where the time goes in v3:
time: 57.5 us; the launch traced here: 57.3 us
  starting transfers between devices  28.9 us (50%)
  waiting for transfers between devices  16.4 us (29%)
  Pallas kernels  10.6 us (18%)
  between operations  1.38 us (2%)
    ppermute x18, starting transfers between devices, spread(): came[d] = lax.ppermute(pieces[d], 'seq', [(i, i ^ d) for i in range(n)])  27.4 us
    ppermute x18, waiting for transfers between devices, spread(): came[d] = lax.ppermute(pieces[d], 'seq', [(i, i ^ d) for i in range(n)])  16.3 us
    pallas_call x9, Pallas kernels, call(): pl.pallas_call(kernel, out_shape=out_shape, in_specs=spaces or [VMEM] * l...  10.6 us
    ppermute x1, starting transfers between devices, exchanged_body(): lax.ppermute(query_grad, 'slide', [(i, (i + step) % sides) for i in range...  1.49 us
  transfers between devices with their start and end apart: 20, of which 7 were waited for; matrix products, arithmetic and copies ran while one was open for 0% of the time, Pallas kernels for 11%

profile of v3, /device:TPU:0, one launch (start us, length us, event | category | flops | bytes accessed | tf_op | source)
XLA Modules:
  0.0 57.3 jit_solution(5409917652117955745)
XLA Ops:
  0.6 1.1 %shard_map.103 = (bf16[400,128]{1,0:T(8,128)(2,1)S(1)}, bf16[400,128]{1,0:T(8,128)(2,1)S(1)}, bf16[400,128]{1,0:T(8,128)(2,1)S(1)}, bf16[400,128]{1,0:T(8,128)(2,1)S(1)}) custom-call(s32[1,2]{1,0:T(1,128)} %mask_ref.1, bf16[1,256,512]{2,1,0:T(8,128)(2,1)} %keys_ref.1, bf16[128,512]{1,0:T(8,128)(2,1)} %latents_ref.1), custom_call_target="tpu_custom_call" | custom-call | flops 1000000 | bytes 802824 | tf_op jit(solution)/shard_map/pallas_call | solution.py:384
  1.7 3.1 %collective-permute-start = (bf16[400,128]{1,0:T(8,128)(2,1)S(1)}, bf16[400,128]{1,0:T(8,128)(2,1)S(1)}, u32[]{:S(2)}, u32[]{:S(2)}) collective-permute-start(bf16[400,128]{1,0:T(8,128)(2,1)S(1)} %get-tuple-element.41), channel_id=1, source_target_pairs={{0,4},{4,0},{8,12},{12,8},{1,5},{5,1},{9,13},{13,9},{2,6},{6,2},{1... | collective-permute-start | bytes 307208 | tf_op jit(solution)/shard_map/ppermute | solution.py:408
  4.8 2.6 %collective-permute-start.1 = (bf16[400,128]{1,0:T(8,128)(2,1)S(1)}, bf16[400,128]{1,0:T(8,128)(2,1)S(1)}, u32[]{:S(2)}, u32[]{:S(2)}) collective-permute-start(bf16[400,128]{1,0:T(8,128)(2,1)S(1)} %get-tuple-element.42), channel_id=1, source_target_pairs={{0,8},{4,12},{8,0},{12,4},{1,9},{5,13},{9,1},{13,5},{2,10},{6,14},... | collective-permute-start | bytes 307208 | tf_op jit(solution)/shard_map/ppermute | solution.py:408
  7.4 0.0 collective-permute-start.2
  8.1 1.8 %shard_map.102 = (bf16[128,128]{1,0:T(8,128)(2,1)S(1)}, bf16[128,128]{1,0:T(8,128)(2,1)S(1)}, bf16[128,128]{1,0:T(8,128)(2,1)S(1)}, bf16[128,128]{1,0:T(8,128)(2...) custom-call(s32[1]{0:T(128)S(6)} %copy.11.count_ref, ...), custom_call_target="tpu_custom_call" | custom-call | flops 134217728 | bytes 1968132 | tf_op jit(solution)/shard_map/pallas_call | solution.py:384
  9.9 1.0 %collective-permute-start.3 = (bf16[128,128]{1,0:T(8,128)(2,1)S(1)}, bf16[128,128]{1,0:T(8,128)(2,1)S(1)}, u32[]{:S(2)}, u32[]{:S(2)}) collective-permute-start(bf16[128,128]{1,0:T(8,128)(2,1)S(1)} %get-tuple-element.47), channel_id=1, source_target_pairs={{0,4},{4,0},{8,12},{12,8},{1,5},{5,1},{9,13},{13,9},{2,6},{6,2},{1... | collective-permute-start | bytes 98312 | tf_op jit(solution)/shard_map/ppermute | solution.py:408
  10.8 1.1 %collective-permute-start.6 = (bf16[256,128]{1,0:T(8,128)(2,1)S(1)}, bf16[256,128]{1,0:T(8,128)(2,1)S(1)}, u32[]{:S(2)}, u32[]{:S(2)}) collective-permute-start(bf16[256,128]{1,0:T(8,128)(2,1)S(1)} %get-tuple-element.53), channel_id=1, source_target_pairs={{0,4},{4,0},{8,12},{12,8},{1,5},{5,1},{9,13},{13,9},{2,6},{6,2},{1... | collective-permute-start | bytes 196616 | tf_op jit(solution)/shard_map/ppermute | solution.py:408
  12.0 3.8 %collective-permute-done.3.refs_1_ = bf16[128,128]{1,0:T(8,128)(2,1)S(1)} collective-permute-done((bf16[128,128]{1,0:T(8,128)(2,1)S(1)}, bf16[128,128]{1,0:T(8,128)(2,1)S(1)}, u32[]{:S(2)}, u32[]{:S(2)}) %collective-permute-start.3) | collective-permute-done | bytes 32800 | tf_op jit(solution)/shard_map/ppermute | solution.py:408
  15.7 0.9 %collective-permute-start.7 = (bf16[256,128]{1,0:T(8,128)(2,1)S(1)}, bf16[256,128]{1,0:T(8,128)(2,1)S(1)}, u32[]{:S(2)}, u32[]{:S(2)}) collective-permute-start(bf16[256,128]{1,0:T(8,128)(2,1)S(1)} %get-tuple-element.54), channel_id=1, source_target_pairs={{0,8},{4,12},{8,0},{12,4},{1,9},{5,13},{9,1},{13,5},{2,10},{6,14},... | collective-permute-start | bytes 196616 | tf_op jit(solution)/shard_map/ppermute | solution.py:408
  16.6 0.0 collective-permute-done.refs_1_
  16.6 1.8 %collective-permute-start.8 = (bf16[256,128]{1,0:T(8,128)(2,1)S(1)}, bf16[256,128]{1,0:T(8,128)(2,1)S(1)}, u32[]{:S(2)}, u32[]{:S(2)}) collective-permute-start(bf16[256,128]{1,0:T(8,128)(2,1)S(1)} %get-tuple-element.55), channel_id=1, source_target_pairs={{0,12},{4,8},{8,4},{12,0},{1,13},{5,9},{9,5},{13,1},{2,14},{6,10},... | collective-permute-start | bytes 196616 | tf_op jit(solution)/shard_map/ppermute | solution.py:408
  18.4 0.0 collective-permute-done.1.refs_2_
  18.4 2.0 %collective-permute-start.4 = (bf16[128,128]{1,0:T(8,128)(2,1)S(1)}, bf16[128,128]{1,0:T(8,128)(2,1)S(1)}, u32[]{:S(2)}, u32[]{:S(2)}) collective-permute-start(bf16[128,128]{1,0:T(8,128)(2,1)S(1)} %get-tuple-element.48), channel_id=1, source_target_pairs={{0,8},{4,12},{8,0},{12,4},{1,9},{5,13},{9,1},{13,5},{2,10},{6,14},... | collective-permute-start | bytes 98312 | tf_op jit(solution)/shard_map/ppermute | solution.py:408
  20.4 0.0 collective-permute-done.2.refs_3_
  20.4 1.1 %collective-permute-start.5 = (bf16[128,128]{1,0:T(8,128)(2,1)S(1)}, bf16[128,128]{1,0:T(8,128)(2,1)S(1)}, u32[]{:S(2)}, u32[]{:S(2)}) collective-permute-start(bf16[128,128]{1,0:T(8,128)(2,1)S(1)} %get-tuple-element.49), channel_id=1, source_target_pairs={{0,12},{4,8},{8,4},{12,0},{1,13},{5,9},{9,5},{13,1},{2,14},{6,10},... | collective-permute-start | bytes 98312 | tf_op jit(solution)/shard_map/ppermute | solution.py:408
  21.6 1.6 %shard_map.104 = (bf16[2,4,256,512]{3,2,1,0:T(8,128)(2,1)S(1)}, f32[2,1,512]{2,1,0:T(1,128)S(1)}, bf16[4,128,256]{2,1,0:T(8,128)(2,1)S(1)}) custom-call(bf16[400,128]{1,0:T(8,128)(2,1)S(1)} %get-tuple-element.40.refs_0_, bf16[400,128]{1,0:T(8,128)(2,1)S(1)} %collective-permute-done.refs_1_, bf16[400,128]{1,0:T(8,128)(2,1)S(1)} %collective-permute-done.1.refs_2_, ...), custom_call_target="tpu_custom_call" | custom-call | flops 134217728 | bytes 2772992 | tf_op jit(solution)/shard_map/pallas_call | solution.py:384
  23.2 1.9 %collective-permute-done.4.refs_2_ = bf16[128,128]{1,0:T(8,128)(2,1)S(1)} collective-permute-done((bf16[128,128]{1,0:T(8,128)(2,1)S(1)}, bf16[128,128]{1,0:T(8,128)(2,1)S(1)}, u32[]{:S(2)}, u32[]{:S(2)}) %collective-permute-start.4) | collective-permute-done | bytes 32800 | tf_op jit(solution)/shard_map/ppermute | solution.py:408
  25.1 1.0 %collective-permute-done.5.refs_3_ = bf16[128,128]{1,0:T(8,128)(2,1)S(1)} collective-permute-done((bf16[128,128]{1,0:T(8,128)(2,1)S(1)}, bf16[128,128]{1,0:T(8,128)(2,1)S(1)}, u32[]{:S(2)}, u32[]{:S(2)}) %collective-permute-start.5) | collective-permute-done | bytes 32800 | tf_op jit(solution)/shard_map/ppermute | solution.py:408
  26.1 0.8 %shard_map.105 = (bf16[128,512]{1,0:T(8,128)(2,1)S(1)}, bf16[256,128]{1,0:T(8,128)(2,1)S(1)}, bf16[256,128]{1,0:T(8,128)(2,1)S(1)}, bf16[256,128]{1,0:T(8,128)(2,1)S(1)}, bf16[256,128]{1,0:T(8,128)(2,1)S(1)}) custom-call(f32[1,512]{1,0:T(1,128)S(1)} %get-tuple-element.39.live_ref, bf16[2,4,256,512]{3,2,1,0:T(8,128)(2,1)S(1)} %get-tuple-element.44.expo_ref, ...), custom_call_target="tpu_custom_call" | custom-call | flops 134217728 | bytes 2627584 | tf_op jit(solution)/shard_map/pallas_call | solution.py:384
  26.9 0.0 copy-start
  27.0 0.0 collective-permute-done.6.refs_5_
  27.0 0.0 collective-permute-done.7.refs_6_
  27.0 0.0 collective-permute-done.8.refs_7_
  27.0 2.6 %shard_map.106 = (bf16[384,128]{1,0:T(8,128)(2,1)S(1)}, bf16[384,128]{1,0:T(8,128)(2,1)S(1)}, bf16[384,128]{1,0:T(8,128)(2,1)S(1)}, bf16[384,128]{1,0:T(8,128)(2,1)S(1)}, bf16[128,512]{1,0:T(8,128)(2,1)S(1)}) custom-call(f32[1,512]{1,0:T(1,128)S(1)} %get-tuple-element.39.live_ref, bf16[2,4,256,512]{3,2,1,0:T(8,128)(2,1)S(1)} %get-tuple-element.44.expo_ref, ...), custom_call_target="tpu_custom_call" | custom-call | flops 536870912 | bytes 3692544 | tf_op jit(solution)/shard_map/pallas_call | solution.py:384
  29.6 0.1 collective-permute-start.9
  29.7 2.1 %collective-permute-start.10 = (bf16[384,128]{1,0:T(8,128)(2,1)S(1)}, bf16[384,128]{1,0:T(8,128)(2,1)S(1)}, u32[]{:S(2)}, u32[]{:S(2)}) collective-permute-start(bf16[384,128]{1,0:T(8,128)(2,1)S(1)} %get-tuple-element.58), channel_id=1, source_target_pairs={{0,8},{4,12},{8,0},{12,4},{1,9},{5,13},{9,1},{13,5},{2,10},{6,14},... | collective-permute-start | bytes 294920 | tf_op jit(solution)/shard_map/ppermute | solution.py:408
  31.8 2.2 %collective-permute-start.11 = (bf16[384,128]{1,0:T(8,128)(2,1)S(1)}, bf16[384,128]{1,0:T(8,128)(2,1)S(1)}, u32[]{:S(2)}, u32[]{:S(2)}) collective-permute-start(bf16[384,128]{1,0:T(8,128)(2,1)S(1)} %get-tuple-element.59), channel_id=1, source_target_pairs={{0,12},{4,8},{8,4},{12,0},{1,13},{5,9},{9,5},{13,1},{2,14},{6,10},... | collective-permute-start | bytes 294920 | tf_op jit(solution)/shard_map/ppermute | solution.py:408
  34.1 1.5 %collective-permute-start.13 = (bf16[128,512]{1,0:T(8,128)(2,1)S(1)}, bf16[128,512]{1,0:T(8,128)(2,1)S(1)}, u32[]{:S(2)}, u32[]{:S(2)}) collective-permute-start(bf16[128,512]{1,0:T(8,128)(2,1)S(1)} %get-tuple-element.62.own_ref), channel_id=1, source_target_pairs={{0,2},{2,0},{1,3},{3,1},{4,6},{6,4},{5,7},{7,5},{8,10},{10,8},{9,1... | collective-permute-start | bytes 393224 | tf_op jit(solution)/shard_map/ppermute | solution.py:471
  35.5 0.4 collective-permute-done.9.refs_1_
  35.9 3.2 %collective-permute-done.10.refs_2_ = bf16[384,128]{1,0:T(8,128)(2,1)S(1)} collective-permute-done((bf16[384,128]{1,0:T(8,128)(2,1)S(1)}, bf16[384,128]{1,0:T(8,128)(2,1)S(1)}, u32[]{:S(2)}, u32[]{:S(2)}) %collective-permute-start.10) | collective-permute-done | bytes 98336 | tf_op jit(solution)/shard_map/ppermute | solution.py:408
  39.2 0.0 collective-permute-done.11.refs_3_
  39.2 0.0 copy-done
  39.2 1.1 %shard_map.107 = (bf16[1,256,512]{2,1,0:T(8,128)(2,1)}, f32[128,512]{1,0:T(8,128)S(1)}, bf16[128,512]{1,0:T(8,128)(2,1)S(1)}) custom-call(bf16[512,1024]{1,0:T(8,128)(2,1)S(1)} %copy-done, bf16[384,128]{1,0:T(8,128)(2,1)S(1)} %get-tuple-element.56.refs_0_, bf16[384,128]{1,0:T(8,128)(2,1)S(1)} %collective-permute-done.9.refs_1_, ...), custom_call_target="tpu_custom_call" | custom-call | flops 134217728 | bytes 2097152 | tf_op jit(solution)/shard_map/pallas_call | solution.py:384
  40.3 0.0 collective-permute-start.12
  40.3 1.6 %collective-permute-start.17 = (bf16[256,128]{1,0:T(8,128)(2,1)S(1)}, bf16[256,128]{1,0:T(8,128)(2,1)S(1)}, u32[]{:S(2)}, u32[]{:S(2)}) collective-permute-start(bf16[256,128]{1,0:T(8,128)(2,1)S(1)} %get-tuple-element.71), channel_id=1, source_target_pairs={{0,4},{4,0},{8,12},{12,8},{1,5},{5,1},{9,13},{13,9},{2,6},{6,2},{1... | collective-permute-start | bytes 196616 | tf_op jit(solution)/shard_map/ppermute | solution.py:408
  41.9 1.1 %collective-permute-start.18 = (bf16[256,128]{1,0:T(8,128)(2,1)S(1)}, bf16[256,128]{1,0:T(8,128)(2,1)S(1)}, u32[]{:S(2)}, u32[]{:S(2)}) collective-permute-start(bf16[256,128]{1,0:T(8,128)(2,1)S(1)} %get-tuple-element.72), channel_id=1, source_target_pairs={{0,8},{4,12},{8,0},{12,4},{1,9},{5,13},{9,1},{13,5},{2,10},{6,14},... | collective-permute-start | bytes 196616 | tf_op jit(solution)/shard_map/ppermute | solution.py:408
  43.0 1.6 %collective-permute-start.19 = (bf16[256,128]{1,0:T(8,128)(2,1)S(1)}, bf16[256,128]{1,0:T(8,128)(2,1)S(1)}, u32[]{:S(2)}, u32[]{:S(2)}) collective-permute-start(bf16[256,128]{1,0:T(8,128)(2,1)S(1)} %get-tuple-element.73), channel_id=1, source_target_pairs={{0,12},{4,8},{8,4},{12,0},{1,13},{5,9},{9,5},{13,1},{2,14},{6,10},... | collective-permute-start | bytes 196616 | tf_op jit(solution)/shard_map/ppermute | solution.py:408
  44.7 0.0 collective-permute-done.13.other_ref
  44.7 0.8 %collective-permute-start.14 = (bf16[128,128]{1,0:T(8,128)(2,1)S(1)}, bf16[128,128]{1,0:T(8,128)(2,1)S(1)}, u32[]{:S(2)}, u32[]{:S(2)}) collective-permute-start(bf16[128,128]{1,0:T(8,128)(2,1)S(1)} %get-tuple-element.64), channel_id=1, source_target_pairs={{0,4},{4,0},{8,12},{12,8},{1,5},{5,1},{9,13},{13,9},{2,6},{6,2},{1... | collective-permute-start | bytes 98312 | tf_op jit(solution)/shard_map/ppermute | solution.py:408
  45.5 0.0 collective-permute-done.17.refs_1_
  45.5 2.2 %collective-permute-start.15 = (bf16[128,128]{1,0:T(8,128)(2,1)S(1)}, bf16[128,128]{1,0:T(8,128)(2,1)S(1)}, u32[]{:S(2)}, u32[]{:S(2)}) collective-permute-start(bf16[128,128]{1,0:T(8,128)(2,1)S(1)} %get-tuple-element.65), channel_id=1, source_target_pairs={{0,8},{4,12},{8,0},{12,4},{1,9},{5,13},{9,1},{13,5},{2,10},{6,14},... | collective-permute-start | bytes 98312 | tf_op jit(solution)/shard_map/ppermute | solution.py:408
  47.7 3.1 %collective-permute-done.18.refs_2_ = bf16[256,128]{1,0:T(8,128)(2,1)S(1)} collective-permute-done((bf16[256,128]{1,0:T(8,128)(2,1)S(1)}, bf16[256,128]{1,0:T(8,128)(2,1)S(1)}, u32[]{:S(2)}, u32[]{:S(2)}) %collective-permute-start.18) | collective-permute-done | bytes 65568 | tf_op jit(solution)/shard_map/ppermute | solution.py:408
  50.7 2.0 %collective-permute-start.16 = (bf16[128,128]{1,0:T(8,128)(2,1)S(1)}, bf16[128,128]{1,0:T(8,128)(2,1)S(1)}, u32[]{:S(2)}, u32[]{:S(2)}) collective-permute-start(bf16[128,128]{1,0:T(8,128)(2,1)S(1)} %get-tuple-element.66), channel_id=1, source_target_pairs={{0,12},{4,8},{8,4},{12,0},{1,13},{5,9},{9,5},{13,1},{2,14},{6,10},... | collective-permute-start | bytes 98312 | tf_op jit(solution)/shard_map/ppermute | solution.py:408
  52.8 0.0 collective-permute-done.19.refs_3_
  52.8 0.8 %shard_map.110 = bf16[1,256,512]{2,1,0:T(8,128)(2,1)} custom-call(bf16[256,128]{1,0:T(8,128)(2,1)S(1)} %get-tuple-element.70.refs_0_, bf16[256,128]{1,0:T(8,128)(2,1)S(1)} %collective-permute-done.17.refs_1_, bf16[256,128]{1,0:T(8,128)(2,1)S(1)} %collective-permute-done.18.refs_2_, bf16[256,128]{1,0:T(8,128)(2,1)S(1)} %collective-permute-done.19.refs_3_), custom_call_target="tpu_custom_call" | custom-call | flops 1000000 | bytes 524288 | tf_op jit(solution)/shard_map/pallas_call | solution.py:384
  53.5 0.0 collective-permute-done.14.refs_1_
  53.5 0.0 collective-permute-done.15.refs_2_
  53.5 2.9 %collective-permute-done.16.refs_3_ = bf16[128,128]{1,0:T(8,128)(2,1)S(1)} collective-permute-done((bf16[128,128]{1,0:T(8,128)(2,1)S(1)}, bf16[128,128]{1,0:T(8,128)(2,1)S(1)}, u32[]{:S(2)}, u32[]{:S(2)}) %collective-permute-start.16) | collective-permute-done | bytes 32800 | tf_op jit(solution)/shard_map/ppermute | solution.py:408
  56.5 0.0 collective-permute-done.12.came_ref
  56.5 0.8 %shard_map.109 = (f32[128,512]{1,0:T(8,128)}, bf16[1,128,512]{2,1,0:T(8,128)(2,1)}) custom-call(f32[128,512]{1,0:T(8,128)S(1)} %get-tuple-element.60.kept_ref, bf16[128,512]{1,0:T(8,128)(2,1)S(1)} %collective-permute-done.12.came_ref, bf16[128,128]{1,0:T(8,128)(2,1)S(1)} %get-tuple-element.63.refs_0_, bf16[128,128]{1,0:T(8,128)(2,1)S(1)} %collective-permute-done.14.refs_1_, ...), custom_call_target="tpu_custom_call" | custom-call | flops 1000000 | bytes 917504 | tf_op jit(solution)/shard_map/pallas_call | solution.py:384
  (1 shorter events, 0.0 us)
Async XLA Ops:
  1.7 14.8 %collective-permute-start = (bf16[400,128]{1,0:T(8,128)(2,1)S(1)}, bf16[400,128]{1,0:T(8,128)(2,1)S(1)}, u32[]{:S(2)}, u32[]{:S(2)}) collective-permute-start(bf16[400,128]{1,0:T(8,128)(2,1)S(1)} %get-tuple-element.41), channel_id=1, source_target_pairs={{0,4},{4,0},{8,12},{12,8},{1,5},{5,1},{9,13},{13,9},{2,6},{6,2},{1... | collective-permute-start | bytes 307208 | tf_op jit(solution)/shard_map/ppermute | solution.py:408
  4.8 13.6 %collective-permute-start.1 = (bf16[400,128]{1,0:T(8,128)(2,1)S(1)}, bf16[400,128]{1,0:T(8,128)(2,1)S(1)}, u32[]{:S(2)}, u32[]{:S(2)}) collective-permute-start(bf16[400,128]{1,0:T(8,128)(2,1)S(1)} %get-tuple-element.42), channel_id=1, source_target_pairs={{0,8},{4,12},{8,0},{12,4},{1,9},{5,13},{9,1},{13,5},{2,10},{6,14},... | collective-permute-start | bytes 307208 | tf_op jit(solution)/shard_map/ppermute | solution.py:408
  7.4 13.0 %collective-permute-start.2 = (bf16[400,128]{1,0:T(8,128)(2,1)S(1)}, bf16[400,128]{1,0:T(8,128)(2,1)S(1)}, u32[]{:S(2)}, u32[]{:S(2)}) collective-permute-start(bf16[400,128]{1,0:T(8,128)(2,1)S(1)} %get-tuple-element.43), channel_id=1, source_target_pairs={{0,12},{4,8},{8,4},{12,0},{1,13},{5,9},{9,5},{13,1},{2,14},{6,10},... | collective-permute-start | bytes 307208 | tf_op jit(solution)/shard_map/ppermute | solution.py:408
  9.9 5.8 %collective-permute-start.3 = (bf16[128,128]{1,0:T(8,128)(2,1)S(1)}, bf16[128,128]{1,0:T(8,128)(2,1)S(1)}, u32[]{:S(2)}, u32[]{:S(2)}) collective-permute-start(bf16[128,128]{1,0:T(8,128)(2,1)S(1)} %get-tuple-element.47), channel_id=1, source_target_pairs={{0,4},{4,0},{8,12},{12,8},{1,5},{5,1},{9,13},{13,9},{2,6},{6,2},{1... | collective-permute-start | bytes 98312 | tf_op jit(solution)/shard_map/ppermute | solution.py:408
  10.8 16.1 %collective-permute-start.6 = (bf16[256,128]{1,0:T(8,128)(2,1)S(1)}, bf16[256,128]{1,0:T(8,128)(2,1)S(1)}, u32[]{:S(2)}, u32[]{:S(2)}) collective-permute-start(bf16[256,128]{1,0:T(8,128)(2,1)S(1)} %get-tuple-element.53), channel_id=1, source_target_pairs={{0,4},{4,0},{8,12},{12,8},{1,5},{5,1},{9,13},{13,9},{2,6},{6,2},{1... | collective-permute-start | bytes 196616 | tf_op jit(solution)/shard_map/ppermute | solution.py:408
  15.7 11.3 %collective-permute-start.7 = (bf16[256,128]{1,0:T(8,128)(2,1)S(1)}, bf16[256,128]{1,0:T(8,128)(2,1)S(1)}, u32[]{:S(2)}, u32[]{:S(2)}) collective-permute-start(bf16[256,128]{1,0:T(8,128)(2,1)S(1)} %get-tuple-element.54), channel_id=1, source_target_pairs={{0,8},{4,12},{8,0},{12,4},{1,9},{5,13},{9,1},{13,5},{2,10},{6,14},... | collective-permute-start | bytes 196616 | tf_op jit(solution)/shard_map/ppermute | solution.py:408
  16.6 10.4 %collective-permute-start.8 = (bf16[256,128]{1,0:T(8,128)(2,1)S(1)}, bf16[256,128]{1,0:T(8,128)(2,1)S(1)}, u32[]{:S(2)}, u32[]{:S(2)}) collective-permute-start(bf16[256,128]{1,0:T(8,128)(2,1)S(1)} %get-tuple-element.55), channel_id=1, source_target_pairs={{0,12},{4,8},{8,4},{12,0},{1,13},{5,9},{9,5},{13,1},{2,14},{6,10},... | collective-permute-start | bytes 196616 | tf_op jit(solution)/shard_map/ppermute | solution.py:408
  18.4 6.7 %collective-permute-start.4 = (bf16[128,128]{1,0:T(8,128)(2,1)S(1)}, bf16[128,128]{1,0:T(8,128)(2,1)S(1)}, u32[]{:S(2)}, u32[]{:S(2)}) collective-permute-start(bf16[128,128]{1,0:T(8,128)(2,1)S(1)} %get-tuple-element.48), channel_id=1, source_target_pairs={{0,8},{4,12},{8,0},{12,4},{1,9},{5,13},{9,1},{13,5},{2,10},{6,14},... | collective-permute-start | bytes 98312 | tf_op jit(solution)/shard_map/ppermute | solution.py:408
  20.4 5.7 %collective-permute-start.5 = (bf16[128,128]{1,0:T(8,128)(2,1)S(1)}, bf16[128,128]{1,0:T(8,128)(2,1)S(1)}, u32[]{:S(2)}, u32[]{:S(2)}) collective-permute-start(bf16[128,128]{1,0:T(8,128)(2,1)S(1)} %get-tuple-element.49), channel_id=1, source_target_pairs={{0,12},{4,8},{8,4},{12,0},{1,13},{5,9},{9,5},{13,1},{2,14},{6,10},... | collective-permute-start | bytes 98312 | tf_op jit(solution)/shard_map/ppermute | solution.py:408
  26.9 12.2 %copy-start = (bf16[512,1024]{1,0:T(8,128)(2,1)S(1)}, bf16[512,1024]{1,0:T(8,128)(2,1)}, u32[]{:S(2)}) copy-start(bf16[512,1024]{1,0:T(8,128)(2,1)} %weight_ref.3) | copy-start | bytes 3145732
  29.6 6.3 %collective-permute-start.9 = (bf16[384,128]{1,0:T(8,128)(2,1)S(1)}, bf16[384,128]{1,0:T(8,128)(2,1)S(1)}, u32[]{:S(2)}, u32[]{:S(2)}) collective-permute-start(bf16[384,128]{1,0:T(8,128)(2,1)S(1)} %get-tuple-element.57), channel_id=1, source_target_pairs={{0,4},{4,0},{8,12},{12,8},{1,5},{5,1},{9,13},{13,9},{2,6},{6,2},{1... | collective-permute-start | bytes 294920 | tf_op jit(solution)/shard_map/ppermute | solution.py:408
  29.7 9.5 %collective-permute-start.10 = (bf16[384,128]{1,0:T(8,128)(2,1)S(1)}, bf16[384,128]{1,0:T(8,128)(2,1)S(1)}, u32[]{:S(2)}, u32[]{:S(2)}) collective-permute-start(bf16[384,128]{1,0:T(8,128)(2,1)S(1)} %get-tuple-element.58), channel_id=1, source_target_pairs={{0,8},{4,12},{8,0},{12,4},{1,9},{5,13},{9,1},{13,5},{2,10},{6,14},... | collective-permute-start | bytes 294920 | tf_op jit(solution)/shard_map/ppermute | solution.py:408
  31.8 7.3 %collective-permute-start.11 = (bf16[384,128]{1,0:T(8,128)(2,1)S(1)}, bf16[384,128]{1,0:T(8,128)(2,1)S(1)}, u32[]{:S(2)}, u32[]{:S(2)}) collective-permute-start(bf16[384,128]{1,0:T(8,128)(2,1)S(1)} %get-tuple-element.59), channel_id=1, source_target_pairs={{0,12},{4,8},{8,4},{12,0},{1,13},{5,9},{9,5},{13,1},{2,14},{6,10},... | collective-permute-start | bytes 294920 | tf_op jit(solution)/shard_map/ppermute | solution.py:408
  34.1 10.6 %collective-permute-start.13 = (bf16[128,512]{1,0:T(8,128)(2,1)S(1)}, bf16[128,512]{1,0:T(8,128)(2,1)S(1)}, u32[]{:S(2)}, u32[]{:S(2)}) collective-permute-start(bf16[128,512]{1,0:T(8,128)(2,1)S(1)} %get-tuple-element.62.own_ref), channel_id=1, source_target_pairs={{0,2},{2,0},{1,3},{3,1},{4,6},{6,4},{5,7},{7,5},{8,10},{10,8},{9,1... | collective-permute-start | bytes 393224 | tf_op jit(solution)/shard_map/ppermute | solution.py:471
  40.3 16.2 %collective-permute-start.12 = (bf16[128,512]{1,0:T(8,128)(2,1)S(1)}, bf16[128,512]{1,0:T(8,128)(2,1)S(1)}, u32[]{:S(2)}, u32[]{:S(2)}) collective-permute-start(bf16[128,512]{1,0:T(8,128)(2,1)S(1)} %get-tuple-element.61), channel_id=1, source_target_pairs={{0,1},{1,0},{2,3},{3,2},{4,5},{5,4},{6,7},{7,6},{8,9},{9,8},{10,11... | collective-permute-start | bytes 393224 | tf_op jit(solution)/shard_map/ppermute | solution.py:494
  40.3 5.2 %collective-permute-start.17 = (bf16[256,128]{1,0:T(8,128)(2,1)S(1)}, bf16[256,128]{1,0:T(8,128)(2,1)S(1)}, u32[]{:S(2)}, u32[]{:S(2)}) collective-permute-start(bf16[256,128]{1,0:T(8,128)(2,1)S(1)} %get-tuple-element.71), channel_id=1, source_target_pairs={{0,4},{4,0},{8,12},{12,8},{1,5},{5,1},{9,13},{13,9},{2,6},{6,2},{1... | collective-permute-start | bytes 196616 | tf_op jit(solution)/shard_map/ppermute | solution.py:408
  41.9 8.8 %collective-permute-start.18 = (bf16[256,128]{1,0:T(8,128)(2,1)S(1)}, bf16[256,128]{1,0:T(8,128)(2,1)S(1)}, u32[]{:S(2)}, u32[]{:S(2)}) collective-permute-start(bf16[256,128]{1,0:T(8,128)(2,1)S(1)} %get-tuple-element.72), channel_id=1, source_target_pairs={{0,8},{4,12},{8,0},{12,4},{1,9},{5,13},{9,1},{13,5},{2,10},{6,14},... | collective-permute-start | bytes 196616 | tf_op jit(solution)/shard_map/ppermute | solution.py:408
  43.0 9.7 %collective-permute-start.19 = (bf16[256,128]{1,0:T(8,128)(2,1)S(1)}, bf16[256,128]{1,0:T(8,128)(2,1)S(1)}, u32[]{:S(2)}, u32[]{:S(2)}) collective-permute-start(bf16[256,128]{1,0:T(8,128)(2,1)S(1)} %get-tuple-element.73), channel_id=1, source_target_pairs={{0,12},{4,8},{8,4},{12,0},{1,13},{5,9},{9,5},{13,1},{2,14},{6,10},... | collective-permute-start | bytes 196616 | tf_op jit(solution)/shard_map/ppermute | solution.py:408
  44.7 8.8 %collective-permute-start.14 = (bf16[128,128]{1,0:T(8,128)(2,1)S(1)}, bf16[128,128]{1,0:T(8,128)(2,1)S(1)}, u32[]{:S(2)}, u32[]{:S(2)}) collective-permute-start(bf16[128,128]{1,0:T(8,128)(2,1)S(1)} %get-tuple-element.64), channel_id=1, source_target_pairs={{0,4},{4,0},{8,12},{12,8},{1,5},{5,1},{9,13},{13,9},{2,6},{6,2},{1... | collective-permute-start | bytes 98312 | tf_op jit(solution)/shard_map/ppermute | solution.py:408
  45.5 8.0 %collective-permute-start.15 = (bf16[128,128]{1,0:T(8,128)(2,1)S(1)}, bf16[128,128]{1,0:T(8,128)(2,1)S(1)}, u32[]{:S(2)}, u32[]{:S(2)}) collective-permute-start(bf16[128,128]{1,0:T(8,128)(2,1)S(1)} %get-tuple-element.65), channel_id=1, source_target_pairs={{0,8},{4,12},{8,0},{12,4},{1,9},{5,13},{9,1},{13,5},{2,10},{6,14},... | collective-permute-start | bytes 98312 | tf_op jit(solution)/shard_map/ppermute | solution.py:408
  50.7 5.7 %collective-permute-start.16 = (bf16[128,128]{1,0:T(8,128)(2,1)S(1)}, bf16[128,128]{1,0:T(8,128)(2,1)S(1)}, u32[]{:S(2)}, u32[]{:S(2)}) collective-permute-start(bf16[128,128]{1,0:T(8,128)(2,1)S(1)} %get-tuple-element.66), channel_id=1, source_target_pairs={{0,12},{4,8},{8,4},{12,0},{1,13},{5,9},{9,5},{13,1},{2,14},{6,10},... | collective-permute-start | bytes 98312 | tf_op jit(solution)/shard_map/ppermute | solution.py:408

commit v4 on v3

--- a/solution.py
+++ b/solution.py
@@ -338,22 +338,30 @@
 
 def pool_kernel(n, weight_ref, *refs):
     k_refs = refs[:n]
-    key_grad_ref, kept_ref, sent_ref = refs[n : n + 3]
+    kept_ref, sent_ref = refs[n : n + 2]
     me, side = lax.axis_index("seq"), lax.axis_index("head")
     width = k_refs[0].shape[1]
-    tiles = key_grad_ref.shape[1]
+    tiles = k_refs[0].shape[0] - width
     half = kept_ref.shape[1]
     kept = jnp.zeros(kept_ref.shape, f32)
     sent = jnp.zeros(sent_ref.shape, f32)
     for d in range(n):
         owner = (me ^ d)
-        key_grad_ref[0, :, lane_block(owner, width)] = k_refs[d][:tiles, :]
         attended = k_refs[d][tiles:, :].astype(f32).T.astype(bf16)
         inputs = lane_block(owner, width)
         kept = kept + dot_nn(attended, weight_ref[inputs, lane_block(side, half)])
         sent = sent + dot_nn(attended, weight_ref[inputs, lane_block(1 - side, half)])
     kept_ref[...] = kept
     sent_ref[...] = sent.astype(bf16)
+
+
+def keys_home_kernel(n, *refs):
+    k_refs, key_grad_ref = refs[:n], refs[n]
+    me = lax.axis_index("seq")
+    width = k_refs[0].shape[1]
+    tiles = key_grad_ref.shape[1]
+    for d in range(n):
+        key_grad_ref[0, :, lane_block(me ^ d, width)] = k_refs[d][:tiles, :]
 
 
 def join_kernel(n, own_ref, other_ref, *outs):
@@ -481,10 +489,9 @@
     (value_grads,) = call(
         functools.partial(values_home_kernel, n), [sds(tile_values.shape, bf16)], c_list, 1e6
     )
-    key_grads, kept, sent = call(
+    kept, sent = call(
         functools.partial(pool_kernel, n),
         [
-            sds(tile_keys.shape, bf16),
             sds((rows, out_width // 2), f32),
             sds((rows, out_width // 2), bf16),
         ],
@@ -492,6 +499,9 @@
         2 * rows * local_width * out_width,
     )
     came = lax.ppermute(sent, "head", [(0, 1), (1, 0)])
+    (key_grads,) = call(
+        functools.partial(keys_home_kernel, n), [sds(tile_keys.shape, bf16)], k_list, 1e6
+    )
     latent_grads, pooled = call(
         functools.partial(last_kernel, n),
         [sds(latents.shape, f32), sds((1, rows, out_width // 2), bf16)],

time: 57.5 us -> 57 us (level)
  waiting for transfers between devices: 16.4 us -> 15.6 us
    ppermute x18, waiting for transfers between devices: 16.3 us -> 15.6 us  [spread(): came[d] = lax.ppermute(pieces[d], 'seq', [(i, i ^ d) for i in range(n)])]
    pallas_call x9 -> x10, Pallas kernels: 10.6 us -> 10.7 us  [call(): pl.pallas_call(kernel, out_shape=out_shape, in_specs=spaces or [VMEM] * l...]
where the time goes in v4:
time: 57 us; the launch traced here: 56.8 us
  starting transfers between devices  29 us (51%)
  waiting for transfers between devices  15.6 us (27%)
  Pallas kernels  10.7 us (19%)
  between operations  1.4 us (2%)
    ppermute x18, starting transfers between devices, spread(): came[d] = lax.ppermute(pieces[d], 'seq', [(i, i ^ d) for i in range(n)])  27.5 us
    ppermute x18, waiting for transfers between devices, spread(): came[d] = lax.ppermute(pieces[d], 'seq', [(i, i ^ d) for i in range(n)])  15.6 us
    pallas_call x10, Pallas kernels, call(): pl.pallas_call(kernel, out_shape=out_shape, in_specs=spaces or [VMEM] * l...  10.7 us
    ppermute x1, starting transfers between devices, exchanged_body(): lax.ppermute(query_grad, 'slide', [(i, (i + step) % sides) for i in range...  1.49 us
  transfers between devices with their start and end apart: 20, of which 7 were waited for; matrix products, arithmetic and copies ran while one was open for 0% of the time, Pallas kernels for 11%

profile of v4, /device:TPU:0, one launch (start us, length us, event | category | flops | bytes accessed | tf_op | source)
XLA Modules:
  0.0 56.8 jit_solution(5678769425780621491)
XLA Ops:
  0.6 1.1 %shard_map.103 = (bf16[400,128]{1,0:T(8,128)(2,1)S(1)}, bf16[400,128]{1,0:T(8,128)(2,1)S(1)}, bf16[400,128]{1,0:T(8,128)(2,1)S(1)}, bf16[400,128]{1,0:T(8,128)(2,1)S(1)}) custom-call(s32[1,2]{1,0:T(1,128)} %mask_ref.1, bf16[1,256,512]{2,1,0:T(8,128)(2,1)} %keys_ref.1, bf16[128,512]{1,0:T(8,128)(2,1)} %latents_ref.1), custom_call_target="tpu_custom_call" | custom-call | flops 1000000 | bytes 802824 | tf_op jit(solution)/shard_map/pallas_call | solution.py:392
  1.7 3.1 %collective-permute-start = (bf16[400,128]{1,0:T(8,128)(2,1)S(1)}, bf16[400,128]{1,0:T(8,128)(2,1)S(1)}, u32[]{:S(2)}, u32[]{:S(2)}) collective-permute-start(bf16[400,128]{1,0:T(8,128)(2,1)S(1)} %get-tuple-element.40), channel_id=1, source_target_pairs={{0,4},{4,0},{8,12},{12,8},{1,5},{5,1},{9,13},{13,9},{2,6},{6,2},{1... | collective-permute-start | bytes 307208 | tf_op jit(solution)/shard_map/ppermute | solution.py:416
  4.8 2.6 %collective-permute-start.1 = (bf16[400,128]{1,0:T(8,128)(2,1)S(1)}, bf16[400,128]{1,0:T(8,128)(2,1)S(1)}, u32[]{:S(2)}, u32[]{:S(2)}) collective-permute-start(bf16[400,128]{1,0:T(8,128)(2,1)S(1)} %get-tuple-element.41), channel_id=1, source_target_pairs={{0,8},{4,12},{8,0},{12,4},{1,9},{5,13},{9,1},{13,5},{2,10},{6,14},... | collective-permute-start | bytes 307208 | tf_op jit(solution)/shard_map/ppermute | solution.py:416
  7.4 0.0 collective-permute-start.2
  8.1 1.8 %shard_map.102 = (bf16[128,128]{1,0:T(8,128)(2,1)S(1)}, bf16[128,128]{1,0:T(8,128)(2,1)S(1)}, bf16[128,128]{1,0:T(8,128)(2,1)S(1)}, bf16[128,128]{1,0:T(8,128)(2...) custom-call(s32[1]{0:T(128)S(6)} %copy.11.count_ref, ...), custom_call_target="tpu_custom_call" | custom-call | flops 134217728 | bytes 1968132 | tf_op jit(solution)/shard_map/pallas_call | solution.py:392
  9.9 1.0 %collective-permute-start.3 = (bf16[128,128]{1,0:T(8,128)(2,1)S(1)}, bf16[128,128]{1,0:T(8,128)(2,1)S(1)}, u32[]{:S(2)}, u32[]{:S(2)}) collective-permute-start(bf16[128,128]{1,0:T(8,128)(2,1)S(1)} %get-tuple-element.46), channel_id=1, source_target_pairs={{0,4},{4,0},{8,12},{12,8},{1,5},{5,1},{9,13},{13,9},{2,6},{6,2},{1... | collective-permute-start | bytes 98312 | tf_op jit(solution)/shard_map/ppermute | solution.py:416
  10.8 1.1 %collective-permute-start.6 = (bf16[256,128]{1,0:T(8,128)(2,1)S(1)}, bf16[256,128]{1,0:T(8,128)(2,1)S(1)}, u32[]{:S(2)}, u32[]{:S(2)}) collective-permute-start(bf16[256,128]{1,0:T(8,128)(2,1)S(1)} %get-tuple-element.52), channel_id=1, source_target_pairs={{0,4},{4,0},{8,12},{12,8},{1,5},{5,1},{9,13},{13,9},{2,6},{6,2},{1... | collective-permute-start | bytes 196616 | tf_op jit(solution)/shard_map/ppermute | solution.py:416
  12.0 3.8 %collective-permute-done.3.refs_1_ = bf16[128,128]{1,0:T(8,128)(2,1)S(1)} collective-permute-done((bf16[128,128]{1,0:T(8,128)(2,1)S(1)}, bf16[128,128]{1,0:T(8,128)(2,1)S(1)}, u32[]{:S(2)}, u32[]{:S(2)}) %collective-permute-start.3) | collective-permute-done | bytes 32800 | tf_op jit(solution)/shard_map/ppermute | solution.py:416
  15.7 0.9 %collective-permute-start.7 = (bf16[256,128]{1,0:T(8,128)(2,1)S(1)}, bf16[256,128]{1,0:T(8,128)(2,1)S(1)}, u32[]{:S(2)}, u32[]{:S(2)}) collective-permute-start(bf16[256,128]{1,0:T(8,128)(2,1)S(1)} %get-tuple-element.53), channel_id=1, source_target_pairs={{0,8},{4,12},{8,0},{12,4},{1,9},{5,13},{9,1},{13,5},{2,10},{6,14},... | collective-permute-start | bytes 196616 | tf_op jit(solution)/shard_map/ppermute | solution.py:416
  16.6 0.0 collective-permute-done.refs_1_
  16.6 1.8 %collective-permute-start.8 = (bf16[256,128]{1,0:T(8,128)(2,1)S(1)}, bf16[256,128]{1,0:T(8,128)(2,1)S(1)}, u32[]{:S(2)}, u32[]{:S(2)}) collective-permute-start(bf16[256,128]{1,0:T(8,128)(2,1)S(1)} %get-tuple-element.54), channel_id=1, source_target_pairs={{0,12},{4,8},{8,4},{12,0},{1,13},{5,9},{9,5},{13,1},{2,14},{6,10},... | collective-permute-start | bytes 196616 | tf_op jit(solution)/shard_map/ppermute | solution.py:416
  18.4 0.0 collective-permute-done.1.refs_2_
  18.4 2.0 %collective-permute-start.4 = (bf16[128,128]{1,0:T(8,128)(2,1)S(1)}, bf16[128,128]{1,0:T(8,128)(2,1)S(1)}, u32[]{:S(2)}, u32[]{:S(2)}) collective-permute-start(bf16[128,128]{1,0:T(8,128)(2,1)S(1)} %get-tuple-element.47), channel_id=1, source_target_pairs={{0,8},{4,12},{8,0},{12,4},{1,9},{5,13},{9,1},{13,5},{2,10},{6,14},... | collective-permute-start | bytes 98312 | tf_op jit(solution)/shard_map/ppermute | solution.py:416
  20.4 0.0 collective-permute-done.2.refs_3_
  20.4 1.1 %collective-permute-start.5 = (bf16[128,128]{1,0:T(8,128)(2,1)S(1)}, bf16[128,128]{1,0:T(8,128)(2,1)S(1)}, u32[]{:S(2)}, u32[]{:S(2)}) collective-permute-start(bf16[128,128]{1,0:T(8,128)(2,1)S(1)} %get-tuple-element.48), channel_id=1, source_target_pairs={{0,12},{4,8},{8,4},{12,0},{1,13},{5,9},{9,5},{13,1},{2,14},{6,10},... | collective-permute-start | bytes 98312 | tf_op jit(solution)/shard_map/ppermute | solution.py:416
  21.6 1.6 %shard_map.104 = (bf16[2,4,256,512]{3,2,1,0:T(8,128)(2,1)S(1)}, f32[2,1,512]{2,1,0:T(1,128)S(1)}, bf16[4,128,256]{2,1,0:T(8,128)(2,1)S(1)}) custom-call(bf16[400,128]{1,0:T(8,128)(2,1)S(1)} %get-tuple-element.39.refs_0_, bf16[400,128]{1,0:T(8,128)(2,1)S(1)} %collective-permute-done.refs_1_, bf16[400,128]{1,0:T(8,128)(2,1)S(1)} %collective-permute-done.1.refs_2_, ...), custom_call_target="tpu_custom_call" | custom-call | flops 134217728 | bytes 2772992 | tf_op jit(solution)/shard_map/pallas_call | solution.py:392
  23.2 1.9 %collective-permute-done.4.refs_2_ = bf16[128,128]{1,0:T(8,128)(2,1)S(1)} collective-permute-done((bf16[128,128]{1,0:T(8,128)(2,1)S(1)}, bf16[128,128]{1,0:T(8,128)(2,1)S(1)}, u32[]{:S(2)}, u32[]{:S(2)}) %collective-permute-start.4) | collective-permute-done | bytes 32800 | tf_op jit(solution)/shard_map/ppermute | solution.py:416
  25.1 1.0 %collective-permute-done.5.refs_3_ = bf16[128,128]{1,0:T(8,128)(2,1)S(1)} collective-permute-done((bf16[128,128]{1,0:T(8,128)(2,1)S(1)}, bf16[128,128]{1,0:T(8,128)(2,1)S(1)}, u32[]{:S(2)}, u32[]{:S(2)}) %collective-permute-start.5) | collective-permute-done | bytes 32800 | tf_op jit(solution)/shard_map/ppermute | solution.py:416
  26.1 0.8 %shard_map.105 = (bf16[128,512]{1,0:T(8,128)(2,1)S(1)}, bf16[256,128]{1,0:T(8,128)(2,1)S(1)}, bf16[256,128]{1,0:T(8,128)(2,1)S(1)}, bf16[256,128]{1,0:T(8,128)(2,1)S(1)}, bf16[256,128]{1,0:T(8,128)(2,1)S(1)}) custom-call(f32[1,512]{1,0:T(1,128)S(1)} %get-tuple-element.38.live_ref, bf16[2,4,256,512]{3,2,1,0:T(8,128)(2,1)S(1)} %get-tuple-element.43.expo_ref, ...), custom_call_target="tpu_custom_call" | custom-call | flops 134217728 | bytes 2627584 | tf_op jit(solution)/shard_map/pallas_call | solution.py:392
  26.9 0.0 copy-start
  27.0 0.0 collective-permute-done.6.refs_5_
  27.0 0.0 collective-permute-done.7.refs_6_
  27.0 0.0 collective-permute-done.8.refs_7_
  27.0 2.6 %shard_map.106 = (bf16[384,128]{1,0:T(8,128)(2,1)S(1)}, bf16[384,128]{1,0:T(8,128)(2,1)S(1)}, bf16[384,128]{1,0:T(8,128)(2,1)S(1)}, bf16[384,128]{1,0:T(8,128)(2,1)S(1)}, bf16[128,512]{1,0:T(8,128)(2,1)S(1)}) custom-call(f32[1,512]{1,0:T(1,128)S(1)} %get-tuple-element.38.live_ref, bf16[2,4,256,512]{3,2,1,0:T(8,128)(2,1)S(1)} %get-tuple-element.43.expo_ref, ...), custom_call_target="tpu_custom_call" | custom-call | flops 536870912 | bytes 3692544 | tf_op jit(solution)/shard_map/pallas_call | solution.py:392
  29.6 0.1 collective-permute-start.9
  29.7 2.1 %collective-permute-start.10 = (bf16[384,128]{1,0:T(8,128)(2,1)S(1)}, bf16[384,128]{1,0:T(8,128)(2,1)S(1)}, u32[]{:S(2)}, u32[]{:S(2)}) collective-permute-start(bf16[384,128]{1,0:T(8,128)(2,1)S(1)} %get-tuple-element.57), channel_id=1, source_target_pairs={{0,8},{4,12},{8,0},{12,4},{1,9},{5,13},{9,1},{13,5},{2,10},{6,14},... | collective-permute-start | bytes 294920 | tf_op jit(solution)/shard_map/ppermute | solution.py:416
  31.8 2.2 %collective-permute-start.11 = (bf16[384,128]{1,0:T(8,128)(2,1)S(1)}, bf16[384,128]{1,0:T(8,128)(2,1)S(1)}, u32[]{:S(2)}, u32[]{:S(2)}) collective-permute-start(bf16[384,128]{1,0:T(8,128)(2,1)S(1)} %get-tuple-element.58), channel_id=1, source_target_pairs={{0,12},{4,8},{8,4},{12,0},{1,13},{5,9},{9,5},{13,1},{2,14},{6,10},... | collective-permute-start | bytes 294920 | tf_op jit(solution)/shard_map/ppermute | solution.py:416
  34.1 1.5 %collective-permute-start.13 = (bf16[128,512]{1,0:T(8,128)(2,1)S(1)}, bf16[128,512]{1,0:T(8,128)(2,1)S(1)}, u32[]{:S(2)}, u32[]{:S(2)}) collective-permute-start(bf16[128,512]{1,0:T(8,128)(2,1)S(1)} %get-tuple-element.61.own_ref), channel_id=1, source_target_pairs={{0,2},{2,0},{1,3},{3,1},{4,6},{6,4},{5,7},{7,5},{8,10},{10,8},{9,1... | collective-permute-start | bytes 393224 | tf_op jit(solution)/shard_map/ppermute | solution.py:479
  35.5 0.4 collective-permute-done.9.refs_1_
  35.9 3.2 %collective-permute-done.10.refs_2_ = bf16[384,128]{1,0:T(8,128)(2,1)S(1)} collective-permute-done((bf16[384,128]{1,0:T(8,128)(2,1)S(1)}, bf16[384,128]{1,0:T(8,128)(2,1)S(1)}, u32[]{:S(2)}, u32[]{:S(2)}) %collective-permute-start.10) | collective-permute-done | bytes 98336 | tf_op jit(solution)/shard_map/ppermute | solution.py:416
  39.2 0.0 collective-permute-done.11.refs_3_
  39.2 0.0 copy-done
  39.2 0.5 shard_map.107
  39.7 0.1 collective-permute-start.12
  39.7 1.7 %collective-permute-start.17 = (bf16[256,128]{1,0:T(8,128)(2,1)S(1)}, bf16[256,128]{1,0:T(8,128)(2,1)S(1)}, u32[]{:S(2)}, u32[]{:S(2)}) collective-permute-start(bf16[256,128]{1,0:T(8,128)(2,1)S(1)} %get-tuple-element.69), channel_id=1, source_target_pairs={{0,4},{4,0},{8,12},{12,8},{1,5},{5,1},{9,13},{13,9},{2,6},{6,2},{1... | collective-permute-start | bytes 196616 | tf_op jit(solution)/shard_map/ppermute | solution.py:416
  41.4 1.1 %collective-permute-start.18 = (bf16[256,128]{1,0:T(8,128)(2,1)S(1)}, bf16[256,128]{1,0:T(8,128)(2,1)S(1)}, u32[]{:S(2)}, u32[]{:S(2)}) collective-permute-start(bf16[256,128]{1,0:T(8,128)(2,1)S(1)} %get-tuple-element.70), channel_id=1, source_target_pairs={{0,8},{4,12},{8,0},{12,4},{1,9},{5,13},{9,1},{13,5},{2,10},{6,14},... | collective-permute-start | bytes 196616 | tf_op jit(solution)/shard_map/ppermute | solution.py:416
  42.5 1.7 %collective-permute-start.19 = (bf16[256,128]{1,0:T(8,128)(2,1)S(1)}, bf16[256,128]{1,0:T(8,128)(2,1)S(1)}, u32[]{:S(2)}, u32[]{:S(2)}) collective-permute-start(bf16[256,128]{1,0:T(8,128)(2,1)S(1)} %get-tuple-element.71), channel_id=1, source_target_pairs={{0,12},{4,8},{8,4},{12,0},{1,13},{5,9},{9,5},{13,1},{2,14},{6,10},... | collective-permute-start | bytes 196616 | tf_op jit(solution)/shard_map/ppermute | solution.py:416
  44.2 0.0 collective-permute-done.13.other_ref
  44.2 0.8 %collective-permute-start.14 = (bf16[128,128]{1,0:T(8,128)(2,1)S(1)}, bf16[128,128]{1,0:T(8,128)(2,1)S(1)}, u32[]{:S(2)}, u32[]{:S(2)}) collective-permute-start(bf16[128,128]{1,0:T(8,128)(2,1)S(1)} %get-tuple-element.63), channel_id=1, source_target_pairs={{0,4},{4,0},{8,12},{12,8},{1,5},{5,1},{9,13},{13,9},{2,6},{6,2},{1... | collective-permute-start | bytes 98312 | tf_op jit(solution)/shard_map/ppermute | solution.py:416
  45.0 0.0 collective-permute-done.17.refs_1_
  45.0 2.2 %collective-permute-start.15 = (bf16[128,128]{1,0:T(8,128)(2,1)S(1)}, bf16[128,128]{1,0:T(8,128)(2,1)S(1)}, u32[]{:S(2)}, u32[]{:S(2)}) collective-permute-start(bf16[128,128]{1,0:T(8,128)(2,1)S(1)} %get-tuple-element.64), channel_id=1, source_target_pairs={{0,8},{4,12},{8,0},{12,4},{1,9},{5,13},{9,1},{13,5},{2,10},{6,14},... | collective-permute-start | bytes 98312 | tf_op jit(solution)/shard_map/ppermute | solution.py:416
  47.2 3.0 %collective-permute-done.18.refs_2_ = bf16[256,128]{1,0:T(8,128)(2,1)S(1)} collective-permute-done((bf16[256,128]{1,0:T(8,128)(2,1)S(1)}, bf16[256,128]{1,0:T(8,128)(2,1)S(1)}, u32[]{:S(2)}, u32[]{:S(2)}) %collective-permute-start.18) | collective-permute-done | bytes 65568 | tf_op jit(solution)/shard_map/ppermute | solution.py:416
  50.2 2.0 %collective-permute-start.16 = (bf16[128,128]{1,0:T(8,128)(2,1)S(1)}, bf16[128,128]{1,0:T(8,128)(2,1)S(1)}, u32[]{:S(2)}, u32[]{:S(2)}) collective-permute-start(bf16[128,128]{1,0:T(8,128)(2,1)S(1)} %get-tuple-element.65), channel_id=1, source_target_pairs={{0,12},{4,8},{8,4},{12,0},{1,13},{5,9},{9,5},{13,1},{2,14},{6,10},... | collective-permute-start | bytes 98312 | tf_op jit(solution)/shard_map/ppermute | solution.py:416
  52.2 0.0 collective-permute-done.19.refs_3_
  52.2 0.8 %shard_map.111 = bf16[1,256,512]{2,1,0:T(8,128)(2,1)} custom-call(bf16[256,128]{1,0:T(8,128)(2,1)S(1)} %get-tuple-element.68.refs_0_, bf16[256,128]{1,0:T(8,128)(2,1)S(1)} %collective-permute-done.17.refs_1_, bf16[256,128]{1,0:T(8,128)(2,1)S(1)} %collective-permute-done.18.refs_2_, bf16[256,128]{1,0:T(8,128)(2,1)S(1)} %collective-permute-done.19.refs_3_), custom_call_target="tpu_custom_call" | custom-call | flops 1000000 | bytes 524288 | tf_op jit(solution)/shard_map/pallas_call | solution.py:392
  52.9 0.8 %shard_map.110 = bf16[1,256,512]{2,1,0:T(8,128)(2,1)} custom-call(bf16[384,128]{1,0:T(8,128)(2,1)S(1)} %get-tuple-element.55.refs_0_, bf16[384,128]{1,0:T(8,128)(2,1)S(1)} %collective-permute-done.9.refs_1_, bf16[384,128]{1,0:T(8,128)(2,1)S(1)} %collective-permute-done.10.refs_2_, bf16[384,128]{1,0:T(8,128)(2,1)S(1)} %collective-permute-done.11.refs_3_), custom_call_target="tpu_custom_call" | custom-call | flops 1000000 | bytes 655360 | tf_op jit(solution)/shard_map/pallas_call | solution.py:392
  53.7 0.0 collective-permute-done.14.refs_1_
  53.7 0.0 collective-permute-done.15.refs_2_
  53.7 2.2 %collective-permute-done.16.refs_3_ = bf16[128,128]{1,0:T(8,128)(2,1)S(1)} collective-permute-done((bf16[128,128]{1,0:T(8,128)(2,1)S(1)}, bf16[128,128]{1,0:T(8,128)(2,1)S(1)}, u32[]{:S(2)}, u32[]{:S(2)}) %collective-permute-start.16) | collective-permute-done | bytes 32800 | tf_op jit(solution)/shard_map/ppermute | solution.py:416
  55.9 0.0 collective-permute-done.12.came_ref
  55.9 0.8 %shard_map.109 = (f32[128,512]{1,0:T(8,128)}, bf16[1,128,512]{2,1,0:T(8,128)(2,1)}) custom-call(f32[128,512]{1,0:T(8,128)S(1)} %get-tuple-element.59.kept_ref, bf16[128,512]{1,0:T(8,128)(2,1)S(1)} %collective-permute-done.12.came_ref, bf16[128,128]{1,0:T(8,128)(2,1)S(1)} %get-tuple-element.62.refs_0_, bf16[128,128]{1,0:T(8,128)(2,1)S(1)} %collective-permute-done.14.refs_1_, ...), custom_call_target="tpu_custom_call" | custom-call | flops 1000000 | bytes 917504 | tf_op jit(solution)/shard_map/pallas_call | solution.py:392
  (1 shorter events, 0.0 us)
Async XLA Ops:
  1.7 14.8 %collective-permute-start = (bf16[400,128]{1,0:T(8,128)(2,1)S(1)}, bf16[400,128]{1,0:T(8,128)(2,1)S(1)}, u32[]{:S(2)}, u32[]{:S(2)}) collective-permute-start(bf16[400,128]{1,0:T(8,128)(2,1)S(1)} %get-tuple-element.40), channel_id=1, source_target_pairs={{0,4},{4,0},{8,12},{12,8},{1,5},{5,1},{9,13},{13,9},{2,6},{6,2},{1... | collective-permute-start | bytes 307208 | tf_op jit(solution)/shard_map/ppermute | solution.py:416
  4.8 13.6 %collective-permute-start.1 = (bf16[400,128]{1,0:T(8,128)(2,1)S(1)}, bf16[400,128]{1,0:T(8,128)(2,1)S(1)}, u32[]{:S(2)}, u32[]{:S(2)}) collective-permute-start(bf16[400,128]{1,0:T(8,128)(2,1)S(1)} %get-tuple-element.41), channel_id=1, source_target_pairs={{0,8},{4,12},{8,0},{12,4},{1,9},{5,13},{9,1},{13,5},{2,10},{6,14},... | collective-permute-start | bytes 307208 | tf_op jit(solution)/shard_map/ppermute | solution.py:416
  7.4 13.0 %collective-permute-start.2 = (bf16[400,128]{1,0:T(8,128)(2,1)S(1)}, bf16[400,128]{1,0:T(8,128)(2,1)S(1)}, u32[]{:S(2)}, u32[]{:S(2)}) collective-permute-start(bf16[400,128]{1,0:T(8,128)(2,1)S(1)} %get-tuple-element.42), channel_id=1, source_target_pairs={{0,12},{4,8},{8,4},{12,0},{1,13},{5,9},{9,5},{13,1},{2,14},{6,10},... | collective-permute-start | bytes 307208 | tf_op jit(solution)/shard_map/ppermute | solution.py:416
  9.9 5.8 %collective-permute-start.3 = (bf16[128,128]{1,0:T(8,128)(2,1)S(1)}, bf16[128,128]{1,0:T(8,128)(2,1)S(1)}, u32[]{:S(2)}, u32[]{:S(2)}) collective-permute-start(bf16[128,128]{1,0:T(8,128)(2,1)S(1)} %get-tuple-element.46), channel_id=1, source_target_pairs={{0,4},{4,0},{8,12},{12,8},{1,5},{5,1},{9,13},{13,9},{2,6},{6,2},{1... | collective-permute-start | bytes 98312 | tf_op jit(solution)/shard_map/ppermute | solution.py:416
  10.8 16.1 %collective-permute-start.6 = (bf16[256,128]{1,0:T(8,128)(2,1)S(1)}, bf16[256,128]{1,0:T(8,128)(2,1)S(1)}, u32[]{:S(2)}, u32[]{:S(2)}) collective-permute-start(bf16[256,128]{1,0:T(8,128)(2,1)S(1)} %get-tuple-element.52), channel_id=1, source_target_pairs={{0,4},{4,0},{8,12},{12,8},{1,5},{5,1},{9,13},{13,9},{2,6},{6,2},{1... | collective-permute-start | bytes 196616 | tf_op jit(solution)/shard_map/ppermute | solution.py:416
  15.7 11.3 %collective-permute-start.7 = (bf16[256,128]{1,0:T(8,128)(2,1)S(1)}, bf16[256,128]{1,0:T(8,128)(2,1)S(1)}, u32[]{:S(2)}, u32[]{:S(2)}) collective-permute-start(bf16[256,128]{1,0:T(8,128)(2,1)S(1)} %get-tuple-element.53), channel_id=1, source_target_pairs={{0,8},{4,12},{8,0},{12,4},{1,9},{5,13},{9,1},{13,5},{2,10},{6,14},... | collective-permute-start | bytes 196616 | tf_op jit(solution)/shard_map/ppermute | solution.py:416
  16.6 10.4 %collective-permute-start.8 = (bf16[256,128]{1,0:T(8,128)(2,1)S(1)}, bf16[256,128]{1,0:T(8,128)(2,1)S(1)}, u32[]{:S(2)}, u32[]{:S(2)}) collective-permute-start(bf16[256,128]{1,0:T(8,128)(2,1)S(1)} %get-tuple-element.54), channel_id=1, source_target_pairs={{0,12},{4,8},{8,4},{12,0},{1,13},{5,9},{9,5},{13,1},{2,14},{6,10},... | collective-permute-start | bytes 196616 | tf_op jit(solution)/shard_map/ppermute | solution.py:416
  18.4 6.7 %collective-permute-start.4 = (bf16[128,128]{1,0:T(8,128)(2,1)S(1)}, bf16[128,128]{1,0:T(8,128)(2,1)S(1)}, u32[]{:S(2)}, u32[]{:S(2)}) collective-permute-start(bf16[128,128]{1,0:T(8,128)(2,1)S(1)} %get-tuple-element.47), channel_id=1, source_target_pairs={{0,8},{4,12},{8,0},{12,4},{1,9},{5,13},{9,1},{13,5},{2,10},{6,14},... | collective-permute-start | bytes 98312 | tf_op jit(solution)/shard_map/ppermute | solution.py:416
  20.4 5.7 %collective-permute-start.5 = (bf16[128,128]{1,0:T(8,128)(2,1)S(1)}, bf16[128,128]{1,0:T(8,128)(2,1)S(1)}, u32[]{:S(2)}, u32[]{:S(2)}) collective-permute-start(bf16[128,128]{1,0:T(8,128)(2,1)S(1)} %get-tuple-element.48), channel_id=1, source_target_pairs={{0,12},{4,8},{8,4},{12,0},{1,13},{5,9},{9,5},{13,1},{2,14},{6,10},... | collective-permute-start | bytes 98312 | tf_op jit(solution)/shard_map/ppermute | solution.py:416
  26.9 12.2 %copy-start = (bf16[512,1024]{1,0:T(8,128)(2,1)S(1)}, bf16[512,1024]{1,0:T(8,128)(2,1)}, u32[]{:S(2)}) copy-start(bf16[512,1024]{1,0:T(8,128)(2,1)} %weight_ref.3) | copy-start | bytes 3145732
  29.6 6.3 %collective-permute-start.9 = (bf16[384,128]{1,0:T(8,128)(2,1)S(1)}, bf16[384,128]{1,0:T(8,128)(2,1)S(1)}, u32[]{:S(2)}, u32[]{:S(2)}) collective-permute-start(bf16[384,128]{1,0:T(8,128)(2,1)S(1)} %get-tuple-element.56), channel_id=1, source_target_pairs={{0,4},{4,0},{8,12},{12,8},{1,5},{5,1},{9,13},{13,9},{2,6},{6,2},{1... | collective-permute-start | bytes 294920 | tf_op jit(solution)/shard_map/ppermute | solution.py:416
  29.7 9.5 %collective-permute-start.10 = (bf16[384,128]{1,0:T(8,128)(2,1)S(1)}, bf16[384,128]{1,0:T(8,128)(2,1)S(1)}, u32[]{:S(2)}, u32[]{:S(2)}) collective-permute-start(bf16[384,128]{1,0:T(8,128)(2,1)S(1)} %get-tuple-element.57), channel_id=1, source_target_pairs={{0,8},{4,12},{8,0},{12,4},{1,9},{5,13},{9,1},{13,5},{2,10},{6,14},... | collective-permute-start | bytes 294920 | tf_op jit(solution)/shard_map/ppermute | solution.py:416
  31.8 7.3 %collective-permute-start.11 = (bf16[384,128]{1,0:T(8,128)(2,1)S(1)}, bf16[384,128]{1,0:T(8,128)(2,1)S(1)}, u32[]{:S(2)}, u32[]{:S(2)}) collective-permute-start(bf16[384,128]{1,0:T(8,128)(2,1)S(1)} %get-tuple-element.58), channel_id=1, source_target_pairs={{0,12},{4,8},{8,4},{12,0},{1,13},{5,9},{9,5},{13,1},{2,14},{6,10},... | collective-permute-start | bytes 294920 | tf_op jit(solution)/shard_map/ppermute | solution.py:416
  34.1 10.1 %collective-permute-start.13 = (bf16[128,512]{1,0:T(8,128)(2,1)S(1)}, bf16[128,512]{1,0:T(8,128)(2,1)S(1)}, u32[]{:S(2)}, u32[]{:S(2)}) collective-permute-start(bf16[128,512]{1,0:T(8,128)(2,1)S(1)} %get-tuple-element.61.own_ref), channel_id=1, source_target_pairs={{0,2},{2,0},{1,3},{3,1},{4,6},{6,4},{5,7},{7,5},{8,10},{10,8},{9,1... | collective-permute-start | bytes 393224 | tf_op jit(solution)/shard_map/ppermute | solution.py:479
  39.7 16.3 %collective-permute-start.12 = (bf16[128,512]{1,0:T(8,128)(2,1)S(1)}, bf16[128,512]{1,0:T(8,128)(2,1)S(1)}, u32[]{:S(2)}, u32[]{:S(2)}) collective-permute-start(bf16[128,512]{1,0:T(8,128)(2,1)S(1)} %get-tuple-element.60), channel_id=1, source_target_pairs={{0,1},{1,0},{2,3},{3,2},{4,5},{5,4},{6,7},{7,6},{8,9},{9,8},{10,11... | collective-permute-start | bytes 393224 | tf_op jit(solution)/shard_map/ppermute | solution.py:501
  39.7 5.3 %collective-permute-start.17 = (bf16[256,128]{1,0:T(8,128)(2,1)S(1)}, bf16[256,128]{1,0:T(8,128)(2,1)S(1)}, u32[]{:S(2)}, u32[]{:S(2)}) collective-permute-start(bf16[256,128]{1,0:T(8,128)(2,1)S(1)} %get-tuple-element.69), channel_id=1, source_target_pairs={{0,4},{4,0},{8,12},{12,8},{1,5},{5,1},{9,13},{13,9},{2,6},{6,2},{1... | collective-permute-start | bytes 196616 | tf_op jit(solution)/shard_map/ppermute | solution.py:416
  41.4 8.8 %collective-permute-start.18 = (bf16[256,128]{1,0:T(8,128)(2,1)S(1)}, bf16[256,128]{1,0:T(8,128)(2,1)S(1)}, u32[]{:S(2)}, u32[]{:S(2)}) collective-permute-start(bf16[256,128]{1,0:T(8,128)(2,1)S(1)} %get-tuple-element.70), channel_id=1, source_target_pairs={{0,8},{4,12},{8,0},{12,4},{1,9},{5,13},{9,1},{13,5},{2,10},{6,14},... | collective-permute-start | bytes 196616 | tf_op jit(solution)/shard_map/ppermute | solution.py:416
  42.5 9.6 %collective-permute-start.19 = (bf16[256,128]{1,0:T(8,128)(2,1)S(1)}, bf16[256,128]{1,0:T(8,128)(2,1)S(1)}, u32[]{:S(2)}, u32[]{:S(2)}) collective-permute-start(bf16[256,128]{1,0:T(8,128)(2,1)S(1)} %get-tuple-element.71), channel_id=1, source_target_pairs={{0,12},{4,8},{8,4},{12,0},{1,13},{5,9},{9,5},{13,1},{2,14},{6,10},... | collective-permute-start | bytes 196616 | tf_op jit(solution)/shard_map/ppermute | solution.py:416
  44.2 9.5 %collective-permute-start.14 = (bf16[128,128]{1,0:T(8,128)(2,1)S(1)}, bf16[128,128]{1,0:T(8,128)(2,1)S(1)}, u32[]{:S(2)}, u32[]{:S(2)}) collective-permute-start(bf16[128,128]{1,0:T(8,128)(2,1)S(1)} %get-tuple-element.63), channel_id=1, source_target_pairs={{0,4},{4,0},{8,12},{12,8},{1,5},{5,1},{9,13},{13,9},{2,6},{6,2},{1... | collective-permute-start | bytes 98312 | tf_op jit(solution)/shard_map/ppermute | solution.py:416
  45.0 8.7 %collective-permute-start.15 = (bf16[128,128]{1,0:T(8,128)(2,1)S(1)}, bf16[128,128]{1,0:T(8,128)(2,1)S(1)}, u32[]{:S(2)}, u32[]{:S(2)}) collective-permute-start(bf16[128,128]{1,0:T(8,128)(2,1)S(1)} %get-tuple-element.64), channel_id=1, source_target_pairs={{0,8},{4,12},{8,0},{12,4},{1,9},{5,13},{9,1},{13,5},{2,10},{6,14},... | collective-permute-start | bytes 98312 | tf_op jit(solution)/shard_map/ppermute | solution.py:416
  50.2 5.7 %collective-permute-start.16 = (bf16[128,128]{1,0:T(8,128)(2,1)S(1)}, bf16[128,128]{1,0:T(8,128)(2,1)S(1)}, u32[]{:S(2)}, u32[]{:S(2)}) collective-permute-start(bf16[128,128]{1,0:T(8,128)(2,1)S(1)} %get-tuple-element.65), channel_id=1, source_target_pairs={{0,12},{4,8},{8,4},{12,0},{1,13},{5,9},{9,5},{13,1},{2,14},{6,10},... | collective-permute-start | bytes 98312 | tf_op jit(solution)/shard_map/ppermute | solution.py:416
